TPU v7x, 8 devices: a whole 2x2x1 slice. The times are simulated.
8 devices in a mesh: dp: 8 (over z, y, x, core).
Axes of the slice: x: 2, y: 2, z: 1, core: 2. Of those that a mesh axis runs over, the one named last changes fastest.
Arguments:
- img_emb: bfloat16 [16384, 640], P('dp')
- txt_emb: bfloat16 [16384, 640], P('dp')
- log_temp: float32 [], replicated
- logit_bias: float32 [], replicated
Outputs:
- output 1: float32 [], replicated
- output 2: float32 [16384, 640], P('dp')
- output 3: float32 [16384, 640], P('dp')
- output 4: float32 [], replicated
- output 5: float32 [], replicated
All inputs are finite; a program needn't handle non-finite values.
Results may differ from a plain program's by a relative error of at most 0.001.
Values are sent between devices in bfloat16 or wider.
A program may use at most 1 GiB of HBM per device.

v0:
```python
import jax
import jax.numpy as jnp
from jax import lax
from jax.sharding import PartitionSpec as P


def normalize_rows(emb):
    emb32 = emb.astype(jnp.float32)
    inv_norm = lax.rsqrt(jnp.sum(emb32 * emb32, axis=-1, keepdims=True))
    return emb32 * inv_norm, inv_norm


def project_back(unit_rows, inv_norm, grad_dir):
    radial = jnp.sum(unit_rows * grad_dir, axis=-1, keepdims=True)
    return (grad_dir - unit_rows * radial) * inv_norm


def pair_terms(img_b, txt_blk, temp_scale, logit_bias, label_signs):
    sim_vals = jnp.einsum('id,jd->ij', img_b, txt_blk, preferred_element_type=jnp.float32)
    logits = temp_scale * sim_vals + logit_bias
    weights = -label_signs * jax.nn.sigmoid(-label_signs * logits)
    weights_b = weights.astype(jnp.bfloat16)
    img_part = jnp.einsum('ij,jd->id', weights_b, txt_blk, preferred_element_type=jnp.float32)
    txt_part = jnp.einsum('ij,id->jd', weights_b, img_b, preferred_element_type=jnp.float32)
    stat_sums = jnp.stack([
        jnp.sum(jax.nn.softplus(-label_signs * logits)),
        jnp.sum(weights),
        jnp.sum(weights * sim_vals),
    ])
    return img_part, txt_part, stat_sums


def solution(mesh):
    group_size = mesh.shape['dp']
    shift_pairs = [(src_dev, (src_dev + 1) % group_size) for src_dev in range(group_size)]

    def local_fn(img_emb, txt_emb, log_temp, logit_bias):
        rows_dev = img_emb.shape[0]
        total_rows = rows_dev * group_size
        img_unit, img_inv = normalize_rows(img_emb)
        txt_unit, txt_inv = normalize_rows(txt_emb)
        img_b = img_unit.astype(jnp.bfloat16)
        txt_b = txt_unit.astype(jnp.bfloat16)
        temp_scale = jnp.exp(log_temp)
        local_ids = jnp.arange(rows_dev)
        diag_signs = jnp.where(local_ids[:, None] == local_ids[None, :], 1.0, -1.0)
        img_acc, txt_acc, stat_sums = pair_terms(img_b, txt_b, temp_scale, logit_bias, diag_signs)

        def visit_step(step_idx, loop_state):
            txt_blk, txt_acc, img_acc, stat_sums = loop_state
            txt_blk = lax.ppermute(txt_blk, 'dp', shift_pairs)
            txt_acc = lax.ppermute(txt_acc, 'dp', shift_pairs)
            img_part, txt_part, new_sums = pair_terms(img_b, txt_blk, temp_scale, logit_bias, -1.0)
            return txt_blk, txt_acc + txt_part, img_acc + img_part, stat_sums + new_sums

        loop_state = lax.fori_loop(0, group_size - 1, visit_step, (txt_b, txt_acc, img_acc, stat_sums))
        txt_acc = lax.ppermute(loop_state[1], 'dp', shift_pairs)
        img_acc = loop_state[2]
        stat_sums = lax.psum(loop_state[3], 'dp') / total_rows
        grad_img = project_back(img_unit, img_inv, temp_scale * img_acc)
        grad_txt = project_back(txt_unit, txt_inv, temp_scale * txt_acc)
        return stat_sums[0], grad_img, grad_txt, temp_scale * stat_sums[2], stat_sums[1]

    return jax.shard_map(
        local_fn,
        mesh=mesh,
        in_specs=(P('dp', None), P('dp', None), P(), P()),
        out_specs=(P(), P('dp', None), P('dp', None), P(), P()),
        check_vma=False,
    )
```

profile of v0, /device:TPU:0, one launch (start us, length us, event | category | flops | bytes accessed | tf_op | source)
XLA Modules:
  0.0 859.4 jit_solution(1909601759590756141)
XLA Ops:
  9.3 23.4 %fusion.12 = (f32[]{:T(128)}, f32[]{:T(128)}, f32[]{:T(128)}, bf16[2048,2048]{1,0:T(8,128)(2,1)S(1)}) fusion(f32[]{:T(128)S(6)} %copy.26, f32[]{:T(128)} %exp.16, bf16[2048,640]{1,0:T(8,128)(2,1)S(1)} %get-tuple-element.148, bf16[2048,640]{1,0:T(8,128)(2,1)S(1)} %get-tuple-element.143), kind=kOutput, calls=%fused_computation.14 | convolution fusion | flops 5456789504 | bytes 13631508 | tf_op jit(solution)/shard_map/id,jd->ij/dot_general | solution.py:19
  51.8 712.5 %while.16 = (s32[]{:T(128)}, bf16[2048,640]{1,0:T(8,128)(2,1)}, f32[2048,640]{1,0:T(8,128)}, f32[2048,640]{1,0:T(8,128)}, f32[3]{0:T(128)S(1)}, /*index=5*/f32[]...) while((s32[]{:T(128)}, bf16[2048,640]{1,0:T(8,128)(2,1)}, f32[2048,640]{1,0:T(8,128)}, ...), condition=%wide.region_9.10_spmd, body=%wide.region_5.9_spmd.sunk | while | flops 16221995008 | bytes 170918224 | solution.py:56
  55.4 29.6 %collective-permute-done = bf16[2048,640]{1,0:T(8,128)(2,1)S(1)} collective-permute-done((bf16[2048,640]{1,0:T(8,128)(2,1)}, bf16[2048,640]{1,0:T(8,128)(2,1)S(1)}, u32[]{:S(2)}, u32[]{:S(2)}) %collective-permute-start) | collective-permute-done | bytes 2621472 | tf_op jit(solution)/shard_map/while/body/eval_jaxpr/ppermute | solution.py:51
  85.0 23.5 %fusion.57 = (f32[]{:T(128)}, f32[]{:T(128)}, f32[]{:T(128)}, f32[2048,2048]{1,0:T(8,128)}) fusion(f32[]{:T(128)} %get-tuple-element.167, f32[]{:T(128)} %get-tuple-element.165, bf16[2048,640]{1,0:T(8,128)(2,1)} %get-tuple-element.166, bf16[2048,640]{1,0:T(8,128)(2,1)S(1)} %collective-permute-done), kind=kOutput, calls=%fused_computation.1.clone.1 | convolution fusion | flops 5431623680 | bytes 22020116 | tf_op jit(solution)/shard_map/while/body/eval_jaxpr/id,jd->ij/dot_general | solution.py:19
  113.0 11.1 %fusion.59 = f32[2048,640]{1,0:T(8,128)S(1)} fusion(f32[2048,640]{1,0:T(8,128)S(1)} %copy-done.3, bf16[2048,640]{1,0:T(8,128)(2,1)S(1)} %collective-permute-done, f32[2048,2048]{1,0:T(8,128)} %get-tuple-element.138, f32[]{:T(128)} %get-tuple-element.167, f32[]{:T(128)} %get-tuple-element.165), kind=kOutput, calls=%fused_computation.9.clone.1 | convolution fusion | flops 5395185664 | bytes 29884424 | tf_op jit(solution)/shard_map/while/body/eval_jaxpr/ij,jd->id/dot_general | solution.py:23
  124.1 17.1 %collective-permute-done.1 = f32[2048,640]{1,0:T(8,128)} collective-permute-done((f32[2048,640]{1,0:T(8,128)}, f32[2048,640]{1,0:T(8,128)}, u32[]{:S(2)}, u32[]{:S(2)}) %collective-permute-start.1) | collective-permute-done | bytes 5242912 | tf_op jit(solution)/shard_map/while/body/eval_jaxpr/ppermute | solution.py:52
  141.2 13.4 %fusion.58 = f32[2048,640]{1,0:T(8,128)} fusion(f32[2048,640]{1,0:T(8,128)} %collective-permute-done.1, bf16[2048,640]{1,0:T(8,128)(2,1)S(1)} %copy-done.7, f32[2048,2048]{1,0:T(8,128)} %get-tuple-element.138, f32[]{:T(128)} %get-tuple-element.167, f32[]{:T(128)} %get-tuple-element.165), kind=kOutput, calls=%fused_computation.10.clone.1 | convolution fusion | flops 5395185664 | bytes 29884424 | tf_op jit(solution)/shard_map/while/body/eval_jaxpr/ij,id->jd/dot_general | solution.py:24
  156.1 30.5 %collective-permute-done = bf16[2048,640]{1,0:T(8,128)(2,1)S(1)} collective-permute-done((bf16[2048,640]{1,0:T(8,128)(2,1)}, bf16[2048,640]{1,0:T(8,128)(2,1)S(1)}, u32[]{:S(2)}, u32[]{:S(2)}) %collective-permute-start) | collective-permute-done | bytes 2621472 | tf_op jit(solution)/shard_map/while/body/eval_jaxpr/ppermute | solution.py:51
  186.6 23.5 %fusion.57 = (f32[]{:T(128)}, f32[]{:T(128)}, f32[]{:T(128)}, f32[2048,2048]{1,0:T(8,128)}) fusion(f32[]{:T(128)} %get-tuple-element.167, f32[]{:T(128)} %get-tuple-element.165, bf16[2048,640]{1,0:T(8,128)(2,1)} %get-tuple-element.166, bf16[2048,640]{1,0:T(8,128)(2,1)S(1)} %collective-permute-done), kind=kOutput, calls=%fused_computation.1.clone.1 | convolution fusion | flops 5431623680 | bytes 22020116 | tf_op jit(solution)/shard_map/while/body/eval_jaxpr/id,jd->ij/dot_general | solution.py:19
  225.7 17.1 %collective-permute-done.1 = f32[2048,640]{1,0:T(8,128)} collective-permute-done((f32[2048,640]{1,0:T(8,128)}, f32[2048,640]{1,0:T(8,128)}, u32[]{:S(2)}, u32[]{:S(2)}) %collective-permute-start.1) | collective-permute-done | bytes 5242912 | tf_op jit(solution)/shard_map/while/body/eval_jaxpr/ppermute | solution.py:52
  242.8 13.4 %fusion.58 = f32[2048,640]{1,0:T(8,128)} fusion(f32[2048,640]{1,0:T(8,128)} %collective-permute-done.1, bf16[2048,640]{1,0:T(8,128)(2,1)S(1)} %copy-done.7, f32[2048,2048]{1,0:T(8,128)} %get-tuple-element.138, f32[]{:T(128)} %get-tuple-element.167, f32[]{:T(128)} %get-tuple-element.165), kind=kOutput, calls=%fused_computation.10.clone.1 | convolution fusion | flops 5395185664 | bytes 29884424 | tf_op jit(solution)/shard_map/while/body/eval_jaxpr/ij,id->jd/dot_general | solution.py:24
  256.8 31.4 %collective-permute-done = bf16[2048,640]{1,0:T(8,128)(2,1)S(1)} collective-permute-done((bf16[2048,640]{1,0:T(8,128)(2,1)}, bf16[2048,640]{1,0:T(8,128)(2,1)S(1)}, u32[]{:S(2)}, u32[]{:S(2)}) %collective-permute-start) | collective-permute-done | bytes 2621472 | tf_op jit(solution)/shard_map/while/body/eval_jaxpr/ppermute | solution.py:51
  288.2 23.5 %fusion.57 = (f32[]{:T(128)}, f32[]{:T(128)}, f32[]{:T(128)}, f32[2048,2048]{1,0:T(8,128)}) fusion(f32[]{:T(128)} %get-tuple-element.167, f32[]{:T(128)} %get-tuple-element.165, bf16[2048,640]{1,0:T(8,128)(2,1)} %get-tuple-element.166, bf16[2048,640]{1,0:T(8,128)(2,1)S(1)} %collective-permute-done), kind=kOutput, calls=%fused_computation.1.clone.1 | convolution fusion | flops 5431623680 | bytes 22020116 | tf_op jit(solution)/shard_map/while/body/eval_jaxpr/id,jd->ij/dot_general | solution.py:19
  327.3 17.1 %collective-permute-done.1 = f32[2048,640]{1,0:T(8,128)} collective-permute-done((f32[2048,640]{1,0:T(8,128)}, f32[2048,640]{1,0:T(8,128)}, u32[]{:S(2)}, u32[]{:S(2)}) %collective-permute-start.1) | collective-permute-done | bytes 5242912 | tf_op jit(solution)/shard_map/while/body/eval_jaxpr/ppermute | solution.py:52
  344.4 13.4 %fusion.58 = f32[2048,640]{1,0:T(8,128)} fusion(f32[2048,640]{1,0:T(8,128)} %collective-permute-done.1, bf16[2048,640]{1,0:T(8,128)(2,1)S(1)} %copy-done.7, f32[2048,2048]{1,0:T(8,128)} %get-tuple-element.138, f32[]{:T(128)} %get-tuple-element.167, f32[]{:T(128)} %get-tuple-element.165), kind=kOutput, calls=%fused_computation.10.clone.1 | convolution fusion | flops 5395185664 | bytes 29884424 | tf_op jit(solution)/shard_map/while/body/eval_jaxpr/ij,id->jd/dot_general | solution.py:24
  357.9 31.9 %collective-permute-done = bf16[2048,640]{1,0:T(8,128)(2,1)S(1)} collective-permute-done((bf16[2048,640]{1,0:T(8,128)(2,1)}, bf16[2048,640]{1,0:T(8,128)(2,1)S(1)}, u32[]{:S(2)}, u32[]{:S(2)}) %collective-permute-start) | collective-permute-done | bytes 2621472 | tf_op jit(solution)/shard_map/while/body/eval_jaxpr/ppermute | solution.py:51
  389.9 23.5 %fusion.57 = (f32[]{:T(128)}, f32[]{:T(128)}, f32[]{:T(128)}, f32[2048,2048]{1,0:T(8,128)}) fusion(f32[]{:T(128)} %get-tuple-element.167, f32[]{:T(128)} %get-tuple-element.165, bf16[2048,640]{1,0:T(8,128)(2,1)} %get-tuple-element.166, bf16[2048,640]{1,0:T(8,128)(2,1)S(1)} %collective-permute-done), kind=kOutput, calls=%fused_computation.1.clone.1 | convolution fusion | flops 5431623680 | bytes 22020116 | tf_op jit(solution)/shard_map/while/body/eval_jaxpr/id,jd->ij/dot_general | solution.py:19
  428.9 17.1 %collective-permute-done.1 = f32[2048,640]{1,0:T(8,128)} collective-permute-done((f32[2048,640]{1,0:T(8,128)}, f32[2048,640]{1,0:T(8,128)}, u32[]{:S(2)}, u32[]{:S(2)}) %collective-permute-start.1) | collective-permute-done | bytes 5242912 | tf_op jit(solution)/shard_map/while/body/eval_jaxpr/ppermute | solution.py:52
  446.0 13.4 %fusion.58 = f32[2048,640]{1,0:T(8,128)} fusion(f32[2048,640]{1,0:T(8,128)} %collective-permute-done.1, bf16[2048,640]{1,0:T(8,128)(2,1)S(1)} %copy-done.7, f32[2048,2048]{1,0:T(8,128)} %get-tuple-element.138, f32[]{:T(128)} %get-tuple-element.167, f32[]{:T(128)} %get-tuple-element.165), kind=kOutput, calls=%fused_computation.10.clone.1 | convolution fusion | flops 5395185664 | bytes 29884424 | tf_op jit(solution)/shard_map/while/body/eval_jaxpr/ij,id->jd/dot_general | solution.py:24
  459.5 31.9 %collective-permute-done = bf16[2048,640]{1,0:T(8,128)(2,1)S(1)} collective-permute-done((bf16[2048,640]{1,0:T(8,128)(2,1)}, bf16[2048,640]{1,0:T(8,128)(2,1)S(1)}, u32[]{:S(2)}, u32[]{:S(2)}) %collective-permute-start) | collective-permute-done | bytes 2621472 | tf_op jit(solution)/shard_map/while/body/eval_jaxpr/ppermute | solution.py:51
  491.5 23.5 %fusion.57 = (f32[]{:T(128)}, f32[]{:T(128)}, f32[]{:T(128)}, f32[2048,2048]{1,0:T(8,128)}) fusion(f32[]{:T(128)} %get-tuple-element.167, f32[]{:T(128)} %get-tuple-element.165, bf16[2048,640]{1,0:T(8,128)(2,1)} %get-tuple-element.166, bf16[2048,640]{1,0:T(8,128)(2,1)S(1)} %collective-permute-done), kind=kOutput, calls=%fused_computation.1.clone.1 | convolution fusion | flops 5431623680 | bytes 22020116 | tf_op jit(solution)/shard_map/while/body/eval_jaxpr/id,jd->ij/dot_general | solution.py:19
  530.5 17.1 %collective-permute-done.1 = f32[2048,640]{1,0:T(8,128)} collective-permute-done((f32[2048,640]{1,0:T(8,128)}, f32[2048,640]{1,0:T(8,128)}, u32[]{:S(2)}, u32[]{:S(2)}) %collective-permute-start.1) | collective-permute-done | bytes 5242912 | tf_op jit(solution)/shard_map/while/body/eval_jaxpr/ppermute | solution.py:52
  547.6 13.4 %fusion.58 = f32[2048,640]{1,0:T(8,128)} fusion(f32[2048,640]{1,0:T(8,128)} %collective-permute-done.1, bf16[2048,640]{1,0:T(8,128)(2,1)S(1)} %copy-done.7, f32[2048,2048]{1,0:T(8,128)} %get-tuple-element.138, f32[]{:T(128)} %get-tuple-element.167, f32[]{:T(128)} %get-tuple-element.165), kind=kOutput, calls=%fused_computation.10.clone.1 | convolution fusion | flops 5395185664 | bytes 29884424 | tf_op jit(solution)/shard_map/while/body/eval_jaxpr/ij,id->jd/dot_general | solution.py:24
  561.1 31.9 %collective-permute-done = bf16[2048,640]{1,0:T(8,128)(2,1)S(1)} collective-permute-done((bf16[2048,640]{1,0:T(8,128)(2,1)}, bf16[2048,640]{1,0:T(8,128)(2,1)S(1)}, u32[]{:S(2)}, u32[]{:S(2)}) %collective-permute-start) | collective-permute-done | bytes 2621472 | tf_op jit(solution)/shard_map/while/body/eval_jaxpr/ppermute | solution.py:51
  593.1 23.5 %fusion.57 = (f32[]{:T(128)}, f32[]{:T(128)}, f32[]{:T(128)}, f32[2048,2048]{1,0:T(8,128)}) fusion(f32[]{:T(128)} %get-tuple-element.167, f32[]{:T(128)} %get-tuple-element.165, bf16[2048,640]{1,0:T(8,128)(2,1)} %get-tuple-element.166, bf16[2048,640]{1,0:T(8,128)(2,1)S(1)} %collective-permute-done), kind=kOutput, calls=%fused_computation.1.clone.1 | convolution fusion | flops 5431623680 | bytes 22020116 | tf_op jit(solution)/shard_map/while/body/eval_jaxpr/id,jd->ij/dot_general | solution.py:19
  632.1 17.1 %collective-permute-done.1 = f32[2048,640]{1,0:T(8,128)} collective-permute-done((f32[2048,640]{1,0:T(8,128)}, f32[2048,640]{1,0:T(8,128)}, u32[]{:S(2)}, u32[]{:S(2)}) %collective-permute-start.1) | collective-permute-done | bytes 5242912 | tf_op jit(solution)/shard_map/while/body/eval_jaxpr/ppermute | solution.py:52
  649.3 13.4 %fusion.58 = f32[2048,640]{1,0:T(8,128)} fusion(f32[2048,640]{1,0:T(8,128)} %collective-permute-done.1, bf16[2048,640]{1,0:T(8,128)(2,1)S(1)} %copy-done.7, f32[2048,2048]{1,0:T(8,128)} %get-tuple-element.138, f32[]{:T(128)} %get-tuple-element.167, f32[]{:T(128)} %get-tuple-element.165), kind=kOutput, calls=%fused_computation.10.clone.1 | convolution fusion | flops 5395185664 | bytes 29884424 | tf_op jit(solution)/shard_map/while/body/eval_jaxpr/ij,id->jd/dot_general | solution.py:24
  662.8 31.9 %collective-permute-done = bf16[2048,640]{1,0:T(8,128)(2,1)S(1)} collective-permute-done((bf16[2048,640]{1,0:T(8,128)(2,1)}, bf16[2048,640]{1,0:T(8,128)(2,1)S(1)}, u32[]{:S(2)}, u32[]{:S(2)}) %collective-permute-start) | collective-permute-done | bytes 2621472 | tf_op jit(solution)/shard_map/while/body/eval_jaxpr/ppermute | solution.py:51
  694.7 23.5 %fusion.57 = (f32[]{:T(128)}, f32[]{:T(128)}, f32[]{:T(128)}, f32[2048,2048]{1,0:T(8,128)}) fusion(f32[]{:T(128)} %get-tuple-element.167, f32[]{:T(128)} %get-tuple-element.165, bf16[2048,640]{1,0:T(8,128)(2,1)} %get-tuple-element.166, bf16[2048,640]{1,0:T(8,128)(2,1)S(1)} %collective-permute-done), kind=kOutput, calls=%fused_computation.1.clone.1 | convolution fusion | flops 5431623680 | bytes 22020116 | tf_op jit(solution)/shard_map/while/body/eval_jaxpr/id,jd->ij/dot_general | solution.py:19
  733.7 17.1 %collective-permute-done.1 = f32[2048,640]{1,0:T(8,128)} collective-permute-done((f32[2048,640]{1,0:T(8,128)}, f32[2048,640]{1,0:T(8,128)}, u32[]{:S(2)}, u32[]{:S(2)}) %collective-permute-start.1) | collective-permute-done | bytes 5242912 | tf_op jit(solution)/shard_map/while/body/eval_jaxpr/ppermute | solution.py:52
  750.9 13.4 %fusion.58 = f32[2048,640]{1,0:T(8,128)} fusion(f32[2048,640]{1,0:T(8,128)} %collective-permute-done.1, bf16[2048,640]{1,0:T(8,128)(2,1)S(1)} %copy-done.7, f32[2048,2048]{1,0:T(8,128)} %get-tuple-element.138, f32[]{:T(128)} %get-tuple-element.167, f32[]{:T(128)} %get-tuple-element.165), kind=kOutput, calls=%fused_computation.10.clone.1 | convolution fusion | flops 5395185664 | bytes 29884424 | tf_op jit(solution)/shard_map/while/body/eval_jaxpr/ij,id->jd/dot_general | solution.py:24
  764.4 76.3 %psum.7 = f32[3]{0:T(128)S(1)} all-reduce(f32[3]{0:T(128)S(1)} %get-tuple-element.49), channel_id=1, replica_groups=mesh['dp'=8] {'dp'}, use_global_device_ids=true, to_apply=%region_10.11 | all-reduce | flops 3 | bytes 24 | tf_op jit(solution)/shard_map/psum | solution.py:59
  (112 shorter events, 146.4 us)
Async XLA Ops:
  9.2 31.8 %copy-start.6 = (bf16[2048,640]{1,0:T(8,128)(2,1)}, bf16[2048,640]{1,0:T(8,128)(2,1)S(1)}, u32[]{:S(2)}) copy-start(bf16[2048,640]{1,0:T(8,128)(2,1)S(1)} %get-tuple-element.148) | copy-start | bytes 7864324
  51.8 790.1 %copy-start.12 = (f32[2048]{0:T(1024)S(1)}, f32[2048]{0:T(1024)}, u32[]{:S(2)}) copy-start(f32[2048]{0:T(1024)} %copy-done.11) | copy-start | bytes 24580
  51.9 33.1 %collective-permute-start = (bf16[2048,640]{1,0:T(8,128)(2,1)}, bf16[2048,640]{1,0:T(8,128)(2,1)S(1)}, u32[]{:S(2)}, u32[]{:S(2)}) collective-permute-start(bf16[2048,640]{1,0:T(8,128)(2,1)} %get-tuple-element.152), channel_id=1, source_target_pairs={{0,1},{1,2},{2,3},{3,4},{4,5},{5,6},{6,7},{7,0}} | collective-permute-start | bytes 7864328 | tf_op jit(solution)/shard_map/while/body/eval_jaxpr/ppermute | solution.py:51
  52.8 88.4 %collective-permute-start.1 = (f32[2048,640]{1,0:T(8,128)}, f32[2048,640]{1,0:T(8,128)}, u32[]{:S(2)}, u32[]{:S(2)}) collective-permute-start(f32[2048,640]{1,0:T(8,128)} %get-tuple-element.153), channel_id=1, source_target_pairs={{0,1},{1,2},{2,3},{3,4},{4,5},{5,6},{6,7},{7,0}} | collective-permute-start | bytes 15728648 | tf_op jit(solution)/shard_map/while/body/eval_jaxpr/ppermute | solution.py:52
  113.0 28.3 %copy-start.7 = (bf16[2048,640]{1,0:T(8,128)(2,1)S(1)}, bf16[2048,640]{1,0:T(8,128)(2,1)}, u32[]{:S(2)}) copy-start(bf16[2048,640]{1,0:T(8,128)(2,1)} %get-tuple-element.166) | copy-start | bytes 7864324 | tf_op jit(solution)/shard_map/while
  124.1 30.6 %copy-start.4 = (f32[2048,640]{1,0:T(8,128)}, f32[2048,640]{1,0:T(8,128)S(1)}, u32[]{:S(2)}) copy-start(f32[2048,640]{1,0:T(8,128)S(1)} %fusion.59) | copy-start | bytes 15728644 | tf_op jit(solution)/shard_map/while
  154.7 32.0 %collective-permute-start = (bf16[2048,640]{1,0:T(8,128)(2,1)}, bf16[2048,640]{1,0:T(8,128)(2,1)S(1)}, u32[]{:S(2)}, u32[]{:S(2)}) collective-permute-start(bf16[2048,640]{1,0:T(8,128)(2,1)} %get-tuple-element.152), channel_id=1, source_target_pairs={{0,1},{1,2},{2,3},{3,4},{4,5},{5,6},{6,7},{7,0}} | collective-permute-start | bytes 7864328 | tf_op jit(solution)/shard_map/while/body/eval_jaxpr/ppermute | solution.py:51
  154.7 88.1 %collective-permute-start.1 = (f32[2048,640]{1,0:T(8,128)}, f32[2048,640]{1,0:T(8,128)}, u32[]{:S(2)}, u32[]{:S(2)}) collective-permute-start(f32[2048,640]{1,0:T(8,128)} %get-tuple-element.153), channel_id=1, source_target_pairs={{0,1},{1,2},{2,3},{3,4},{4,5},{5,6},{6,7},{7,0}} | collective-permute-start | bytes 15728648 | tf_op jit(solution)/shard_map/while/body/eval_jaxpr/ppermute | solution.py:52
  214.6 28.3 %copy-start.7 = (bf16[2048,640]{1,0:T(8,128)(2,1)S(1)}, bf16[2048,640]{1,0:T(8,128)(2,1)}, u32[]{:S(2)}) copy-start(bf16[2048,640]{1,0:T(8,128)(2,1)} %get-tuple-element.166) | copy-start | bytes 7864324 | tf_op jit(solution)/shard_map/while
  225.7 30.6 %copy-start.4 = (f32[2048,640]{1,0:T(8,128)}, f32[2048,640]{1,0:T(8,128)S(1)}, u32[]{:S(2)}) copy-start(f32[2048,640]{1,0:T(8,128)S(1)} %fusion.59) | copy-start | bytes 15728644 | tf_op jit(solution)/shard_map/while
  256.3 32.0 %collective-permute-start = (bf16[2048,640]{1,0:T(8,128)(2,1)}, bf16[2048,640]{1,0:T(8,128)(2,1)S(1)}, u32[]{:S(2)}, u32[]{:S(2)}) collective-permute-start(bf16[2048,640]{1,0:T(8,128)(2,1)} %get-tuple-element.152), channel_id=1, source_target_pairs={{0,1},{1,2},{2,3},{3,4},{4,5},{5,6},{6,7},{7,0}} | collective-permute-start | bytes 7864328 | tf_op jit(solution)/shard_map/while/body/eval_jaxpr/ppermute | solution.py:51
  256.3 88.1 %collective-permute-start.1 = (f32[2048,640]{1,0:T(8,128)}, f32[2048,640]{1,0:T(8,128)}, u32[]{:S(2)}, u32[]{:S(2)}) collective-permute-start(f32[2048,640]{1,0:T(8,128)} %get-tuple-element.153), channel_id=1, source_target_pairs={{0,1},{1,2},{2,3},{3,4},{4,5},{5,6},{6,7},{7,0}} | collective-permute-start | bytes 15728648 | tf_op jit(solution)/shard_map/while/body/eval_jaxpr/ppermute | solution.py:52
  316.2 28.3 %copy-start.7 = (bf16[2048,640]{1,0:T(8,128)(2,1)S(1)}, bf16[2048,640]{1,0:T(8,128)(2,1)}, u32[]{:S(2)}) copy-start(bf16[2048,640]{1,0:T(8,128)(2,1)} %get-tuple-element.166) | copy-start | bytes 7864324 | tf_op jit(solution)/shard_map/while
  327.3 30.6 %copy-start.4 = (f32[2048,640]{1,0:T(8,128)}, f32[2048,640]{1,0:T(8,128)S(1)}, u32[]{:S(2)}) copy-start(f32[2048,640]{1,0:T(8,128)S(1)} %fusion.59) | copy-start | bytes 15728644 | tf_op jit(solution)/shard_map/while
  357.9 32.0 %collective-permute-start = (bf16[2048,640]{1,0:T(8,128)(2,1)}, bf16[2048,640]{1,0:T(8,128)(2,1)S(1)}, u32[]{:S(2)}, u32[]{:S(2)}) collective-permute-start(bf16[2048,640]{1,0:T(8,128)(2,1)} %get-tuple-element.152), channel_id=1, source_target_pairs={{0,1},{1,2},{2,3},{3,4},{4,5},{5,6},{6,7},{7,0}} | collective-permute-start | bytes 7864328 | tf_op jit(solution)/shard_map/while/body/eval_jaxpr/ppermute | solution.py:51
  357.9 88.1 %collective-permute-start.1 = (f32[2048,640]{1,0:T(8,128)}, f32[2048,640]{1,0:T(8,128)}, u32[]{:S(2)}, u32[]{:S(2)}) collective-permute-start(f32[2048,640]{1,0:T(8,128)} %get-tuple-element.153), channel_id=1, source_target_pairs={{0,1},{1,2},{2,3},{3,4},{4,5},{5,6},{6,7},{7,0}} | collective-permute-start | bytes 15728648 | tf_op jit(solution)/shard_map/while/body/eval_jaxpr/ppermute | solution.py:52
  417.8 28.3 %copy-start.7 = (bf16[2048,640]{1,0:T(8,128)(2,1)S(1)}, bf16[2048,640]{1,0:T(8,128)(2,1)}, u32[]{:S(2)}) copy-start(bf16[2048,640]{1,0:T(8,128)(2,1)} %get-tuple-element.166) | copy-start | bytes 7864324 | tf_op jit(solution)/shard_map/while
  428.9 30.6 %copy-start.4 = (f32[2048,640]{1,0:T(8,128)}, f32[2048,640]{1,0:T(8,128)S(1)}, u32[]{:S(2)}) copy-start(f32[2048,640]{1,0:T(8,128)S(1)} %fusion.59) | copy-start | bytes 15728644 | tf_op jit(solution)/shard_map/while
  459.5 32.0 %collective-permute-start = (bf16[2048,640]{1,0:T(8,128)(2,1)}, bf16[2048,640]{1,0:T(8,128)(2,1)S(1)}, u32[]{:S(2)}, u32[]{:S(2)}) collective-permute-start(bf16[2048,640]{1,0:T(8,128)(2,1)} %get-tuple-element.152), channel_id=1, source_target_pairs={{0,1},{1,2},{2,3},{3,4},{4,5},{5,6},{6,7},{7,0}} | collective-permute-start | bytes 7864328 | tf_op jit(solution)/shard_map/while/body/eval_jaxpr/ppermute | solution.py:51
  459.5 88.1 %collective-permute-start.1 = (f32[2048,640]{1,0:T(8,128)}, f32[2048,640]{1,0:T(8,128)}, u32[]{:S(2)}, u32[]{:S(2)}) collective-permute-start(f32[2048,640]{1,0:T(8,128)} %get-tuple-element.153), channel_id=1, source_target_pairs={{0,1},{1,2},{2,3},{3,4},{4,5},{5,6},{6,7},{7,0}} | collective-permute-start | bytes 15728648 | tf_op jit(solution)/shard_map/while/body/eval_jaxpr/ppermute | solution.py:52
  519.4 28.3 %copy-start.7 = (bf16[2048,640]{1,0:T(8,128)(2,1)S(1)}, bf16[2048,640]{1,0:T(8,128)(2,1)}, u32[]{:S(2)}) copy-start(bf16[2048,640]{1,0:T(8,128)(2,1)} %get-tuple-element.166) | copy-start | bytes 7864324 | tf_op jit(solution)/shard_map/while
  530.5 30.6 %copy-start.4 = (f32[2048,640]{1,0:T(8,128)}, f32[2048,640]{1,0:T(8,128)S(1)}, u32[]{:S(2)}) copy-start(f32[2048,640]{1,0:T(8,128)S(1)} %fusion.59) | copy-start | bytes 15728644 | tf_op jit(solution)/shard_map/while
  561.1 32.0 %collective-permute-start = (bf16[2048,640]{1,0:T(8,128)(2,1)}, bf16[2048,640]{1,0:T(8,128)(2,1)S(1)}, u32[]{:S(2)}, u32[]{:S(2)}) collective-permute-start(bf16[2048,640]{1,0:T(8,128)(2,1)} %get-tuple-element.152), channel_id=1, source_target_pairs={{0,1},{1,2},{2,3},{3,4},{4,5},{5,6},{6,7},{7,0}} | collective-permute-start | bytes 7864328 | tf_op jit(solution)/shard_map/while/body/eval_jaxpr/ppermute | solution.py:51
  561.1 88.1 %collective-permute-start.1 = (f32[2048,640]{1,0:T(8,128)}, f32[2048,640]{1,0:T(8,128)}, u32[]{:S(2)}, u32[]{:S(2)}) collective-permute-start(f32[2048,640]{1,0:T(8,128)} %get-tuple-element.153), channel_id=1, source_target_pairs={{0,1},{1,2},{2,3},{3,4},{4,5},{5,6},{6,7},{7,0}} | collective-permute-start | bytes 15728648 | tf_op jit(solution)/shard_map/while/body/eval_jaxpr/ppermute | solution.py:52
  621.0 28.3 %copy-start.7 = (bf16[2048,640]{1,0:T(8,128)(2,1)S(1)}, bf16[2048,640]{1,0:T(8,128)(2,1)}, u32[]{:S(2)}) copy-start(bf16[2048,640]{1,0:T(8,128)(2,1)} %get-tuple-element.166) | copy-start | bytes 7864324 | tf_op jit(solution)/shard_map/while
  632.1 30.6 %copy-start.4 = (f32[2048,640]{1,0:T(8,128)}, f32[2048,640]{1,0:T(8,128)S(1)}, u32[]{:S(2)}) copy-start(f32[2048,640]{1,0:T(8,128)S(1)} %fusion.59) | copy-start | bytes 15728644 | tf_op jit(solution)/shard_map/while
  662.7 32.0 %collective-permute-start = (bf16[2048,640]{1,0:T(8,128)(2,1)}, bf16[2048,640]{1,0:T(8,128)(2,1)S(1)}, u32[]{:S(2)}, u32[]{:S(2)}) collective-permute-start(bf16[2048,640]{1,0:T(8,128)(2,1)} %get-tuple-element.152), channel_id=1, source_target_pairs={{0,1},{1,2},{2,3},{3,4},{4,5},{5,6},{6,7},{7,0}} | collective-permute-start | bytes 7864328 | tf_op jit(solution)/shard_map/while/body/eval_jaxpr/ppermute | solution.py:51
  662.7 88.1 %collective-permute-start.1 = (f32[2048,640]{1,0:T(8,128)}, f32[2048,640]{1,0:T(8,128)}, u32[]{:S(2)}, u32[]{:S(2)}) collective-permute-start(f32[2048,640]{1,0:T(8,128)} %get-tuple-element.153), channel_id=1, source_target_pairs={{0,1},{1,2},{2,3},{3,4},{4,5},{5,6},{6,7},{7,0}} | collective-permute-start | bytes 15728648 | tf_op jit(solution)/shard_map/while/body/eval_jaxpr/ppermute | solution.py:52
  722.6 28.3 %copy-start.7 = (bf16[2048,640]{1,0:T(8,128)(2,1)S(1)}, bf16[2048,640]{1,0:T(8,128)(2,1)}, u32[]{:S(2)}) copy-start(bf16[2048,640]{1,0:T(8,128)(2,1)} %get-tuple-element.166) | copy-start | bytes 7864324 | tf_op jit(solution)/shard_map/while
  733.7 30.6 %copy-start.4 = (f32[2048,640]{1,0:T(8,128)}, f32[2048,640]{1,0:T(8,128)S(1)}, u32[]{:S(2)}) copy-start(f32[2048,640]{1,0:T(8,128)S(1)} %fusion.59) | copy-start | bytes 15728644 | tf_op jit(solution)/shard_map/while
  764.3 82.3 %copy-start.1 = (bf16[2048,640]{1,0:T(8,128)(2,1)S(1)}, bf16[2048,640]{1,0:T(8,128)(2,1)}, u32[]{:S(2)}) copy-start(bf16[2048,640]{1,0:T(8,128)(2,1)} %param.6) | copy-start | bytes 7864324
  764.3 85.4 %collective-permute-start.2 = (f32[2048,640]{1,0:T(8,128)}, f32[2048,640]{1,0:T(8,128)}, u32[]{:S(2)}, u32[]{:S(2)}) collective-permute-start(f32[2048,640]{1,0:T(8,128)} %get-tuple-element.51), channel_id=1, source_target_pairs={{0,1},{1,2},{2,3},{3,4},{4,5},{5,6},{6,7},{7,0}} | collective-permute-start | bytes 15728648 | tf_op jit(solution)/shard_map/ppermute | solution.py:57
  (14 other events, 81.1 us)
where the time goes:
time: 860 us; the launch traced here: 859 us
  matrix products  377 us (44%)
  waiting for transfers between devices  339 us (39%)
  blocking collectives  76.3 us (9%)
  other arithmetic  45.4 us (5%)
  local copies, waits for them, and re-layouts  11.7 us (1%)
    ppermute x7, waiting for transfers between devices, visit_step(): txt_blk = lax.ppermute(txt_blk, 'dp', shift_pairs)  219 us
    dot_general x8, matrix products, pair_terms(): jnp.einsum('id,jd->ij', img_b, txt_blk, preferred_element_type=jnp.float32)  188 us
    ppermute x7, waiting for transfers between devices, visit_step(): txt_acc = lax.ppermute(txt_acc, 'dp', shift_pairs)  120 us
    dot_general x8, matrix products, pair_terms(): jnp.einsum('ij,id->jd', weights_b, img_b, preferred_element_type=jnp.floa...  103 us
    dot_general x8, matrix products, pair_terms(): jnp.einsum('ij,jd->id', weights_b, txt_blk, preferred_element_type=jnp.fl...  86.1 us
    psum x1, blocking collectives, local_fn(): stat_sums = lax.psum(loop_state[3], 'dp') / total_rows  76.3 us
    add x7, other arithmetic, visit_step(): stat_sums + new_sums  19.8 us
  transfers between devices with their start and end apart: 15, of which 14 were waited for; matrix products, arithmetic and copies ran while one was open for 33% of the time, Pallas kernels for 0%

commit v1 on v0

v1 whole, which is shorter than its diff:
```python
import functools

import jax
import jax.numpy as jnp
from jax import lax
from jax.experimental import pallas as pl
from jax.experimental.pallas import tpu as pltpu
from jax.sharding import PartitionSpec as P

F32, BF16 = jnp.float32, jnp.bfloat16
MESH = pl.DeviceIdType.MESH
LOG2E = 1.4426950408889634
LN2 = 0.6931471805599453
CLAMP = 64.0
TR, TC, LANE = 512, 1024, 128
HALF = TC // 2
HR, HC = 64, 256
SEG = 4

ORDER = [
    (0, 0), (1, 1), (2, 2), (3, 3), (0, 1), (1, 0), (0, 2), (2, 0),
    (4, 0), (4, 1), (0, 4), (1, 4), (2, 4), (3, 4), (4, 4), (4, 2),
    (4, 3), (4, 5), (5, 4), (5, 0), (6, 4), (5, 1), (4, 6), (5, 2),
    (7, 4), (5, 3), (4, 7), (5, 5), (5, 6), (5, 7), (0, 5), (1, 5),
    (2, 5), (3, 5), (6, 5), (7, 5), (6, 0), (6, 1), (6, 2), (6, 3),
    (6, 6), (6, 7), (0, 6), (1, 6), (2, 6), (3, 6), (7, 6), (7, 7),
    (7, 0), (7, 1), (7, 2), (7, 3), (0, 7), (1, 7), (2, 7), (3, 7),
    (0, 3), (3, 0), (1, 2), (2, 1), (1, 3), (3, 1), (2, 3), (3, 2),
]
NT = len(ORDER)
DIAG_TRIPS = 2
FORWARD_TRIP = (3, 6, 9, 11)


def tile_at(trip, parity):
    if isinstance(trip, int):
        return ORDER[2 * trip + parity]
    code = jnp.int32(8 * ORDER[parity][0] + ORDER[parity][1])
    for k in range(1, NT // 2):
        r, g = ORDER[2 * k + parity]
        code = jnp.where(trip == k, 8 * r + g, code)
    return code // 8, code % 8


def last_use(match):
    return max(t for t, rg in enumerate(ORDER) if match(*rg))


def first_use(match):
    return min(t for t, rg in enumerate(ORDER) if match(*rg))


def kernel(scal, x_hbm, xt_hbm, yt_hbm, u_out, v_out, u_in, v_in, vp_in, stats, x_all, xt_all, yt_all, u_all, v_all,
           s0, s1, h0, h1, v_part, loc_sem, img_s, img_r, own_s, own_r, col_s, col_r, fwd_s, fwd_r, u_s, u_r,
           q_s, q_r, v_s, v_r, b_s, b_r, out_sem, free_sem):
    me = lax.axis_index('dp')
    core_nbr, row_nbr, col_nbr = me ^ 1, me ^ 2, me ^ 4
    dim = u_all.shape[0]
    rows = x_hbm.shape[1]
    nblk = rows // LANE
    cblk = HALF // LANE
    kblk = x_hbm.shape[0]

    barrier = pltpu.get_barrier_semaphore()
    for nbr in (core_nbr, row_nbr, col_nbr):
        pl.semaphore_signal(barrier, inc=1, device_id=(nbr,), device_id_type=MESH)

    def remote(src, dst, s, r, k, dev):
        return pltpu.make_async_remote_copy(src_ref=src, dst_ref=dst, send_sem=s.at[k], recv_sem=r.at[k],
                                            device_id=(dev,), device_id_type=MESH)

    def img(k):
        return remote(x_hbm.at[:, pl.ds(k * TR, TR)], x_all.at[:, pl.ds(rows + k * TR, TR)], img_s, img_r, k, row_nbr)

    def own(k):
        return remote(yt_hbm.at[pl.ds(k * cblk, cblk)], yt_all.at[pl.ds(k * 2 * cblk + cblk, cblk)], own_s, own_r, k,
                      core_nbr)

    def col(k):
        return remote(yt_hbm.at[pl.ds(k * cblk, cblk)], yt_all.at[pl.ds((SEG + k) * 2 * cblk, cblk)], col_s, col_r, k,
                      col_nbr)

    def fwd(k):
        return remote(yt_all.at[pl.ds((SEG + k) * 2 * cblk, cblk)], yt_all.at[pl.ds((SEG + k) * 2 * cblk + cblk, cblk)],
                      fwd_s, fwd_r, k, core_nbr)

    def u_send(k):
        return remote(u_all.at[:, pl.ds(rows + k * TR, TR)], u_in.at[:, pl.ds(k * TR, TR)], u_s, u_r, k, row_nbr)

    def q_send(k):
        return remote(v_all.at[:, pl.ds((SEG + k) * TC + HALF, HALF)], v_part.at[k % 2], q_s, q_r, k, core_nbr)

    def v_send(k):
        return remote(v_all.at[:, pl.ds((SEG + k) * TC, HALF)], v_in.at[:, pl.ds(k * HALF, HALF)], v_s, v_r, k, col_nbr)

    def b_send(k):
        return remote(v_all.at[:, pl.ds(k * TC + HALF, HALF)], vp_in.at[:, pl.ds(k * HALF, HALF)], b_s, b_r, k, core_nbr)

    def load(k):
        if k < SEG:
            return pltpu.make_async_copy(yt_hbm.at[pl.ds(k * cblk, cblk)], yt_all.at[pl.ds(k * 2 * cblk, cblk)],
                                         loc_sem.at[k])
        if k == SEG:
            return pltpu.make_async_copy(x_hbm, x_all.at[:, pl.ds(0, rows)], loc_sem.at[k])
        return pltpu.make_async_copy(xt_hbm, xt_all.at[pl.ds(0, nblk)], loc_sem.at[k])

    def store(k):
        if k < SEG:
            return pltpu.make_async_copy(v_all.at[:, pl.ds(k * TC, HALF)], v_out.at[:, pl.ds(k * HALF, HALF)],
                                         out_sem.at[k])
        return pltpu.make_async_copy(u_all.at[:, pl.ds(0, rows)], u_out, out_sem.at[k])

    for k in (SEG, 0, 1, 2, 3, SEG + 1):
        load(k).start()
    pl.semaphore_wait(barrier, 3)
    for k in range(SEG):
        own(k).start()
        img(k).start()
        col(k).start()

    scale2, bias2 = scal[0], scal[1]
    stats[...] = jnp.zeros_like(stats)
    u_all[...] = jnp.zeros_like(u_all)
    v_all[...] = jnp.zeros_like(v_all)
    sim, wgt = (s0, s1), (h0, h1)

    def cat(ref, first, count, rows_at):
        return jnp.concatenate([ref[first + q, rows_at, :] for q in range(count)], axis=1)

    def aligned(start, size):
        return pl.ds(start if isinstance(start, int) else pl.multiple_of(start, size), size)

    every = pl.ds(0, dim)

    def sim_pieces(trip, slot):
        r, g = tile_at(trip, slot)

        def piece(k):
            texts = cat(yt_all, g * 2 * cblk + k * cblk, cblk, every)
            images = cat(x_all, 0, kblk, aligned(r * TR, TR))
            sim[slot][:, k * HALF:(k + 1) * HALF] = jnp.dot(images, texts, preferred_element_type=F32)

        return [functools.partial(piece, k) for k in range(2)]

    def grad_pieces(trip, slot):
        r, g = tile_at(trip, slot)

        def img_piece():
            u_all[:, aligned(r * TR, TR)] += lax.dot_general(
                cat(yt_all, g * 2 * cblk, 2 * cblk, every), cat(wgt[slot], 0, 2 * cblk, pl.ds(0, TR)),
                (((1,), (1,)), ((), ())), preferred_element_type=F32)

        def txt_piece(k):
            v_all[:, aligned(g * TC + k * HALF, HALF)] += jnp.dot(
                cat(xt_all, r * (TR // LANE), TR // LANE, every), cat(wgt[slot], k * cblk, cblk, pl.ds(0, TR)),
                preferred_element_type=F32)

        return [img_piece] + [functools.partial(txt_piece, k) for k in range(2)]

    def weight_pieces(trip, slot, count, diag):
        blocks = [(r, c) for r in range(0, TR, HR) for c in range(0, TC, HC)]
        per = -(-len(blocks) // count)
        sums = [None] * 4
        if diag:
            tr, tg = tile_at(trip, slot)
            offset = jnp.where(tr == tg, 0, 4 * TC)
            lag = lax.broadcasted_iota(jnp.int32, (HR, HC), 1) - lax.broadcasted_iota(jnp.int32, (HR, HC), 0)

        def fold(q):
            return jnp.sum(q.reshape(HR // 8, 8, HC), axis=0)

        def piece(k):
            for r, c in blocks[k * per:(k + 1) * per]:
                on_diag = diag and c < HALF and r < c + HC and c < r + HR
                s = sim[slot][r:r + HR, c:c + HC]
                logit2 = s * scale2 + bias2
                if on_diag:
                    same = lag == r - c + offset
                    logit2 = jnp.where(same, -logit2, logit2)
                clamped = jnp.minimum(logit2, CLAMP)
                e = jnp.exp2(clamped)
                v = 1.0 + e
                inv = 1.0 / v
                h = e * inv
                kept = (v - 1.0) * inv
                if on_diag:
                    signed = jnp.where(same, -h, h)
                    kept = kept - h + signed
                    h = signed
                hb = h.astype(BF16)
                for cc in range(0, HC, LANE):
                    wgt[slot][(c + cc) // LANE, r:r + HR, :] = hb[:, cc:cc + LANE]
                for q, part in enumerate((jnp.log2(v) + (logit2 - clamped), kept, h, h * s)):
                    part = fold(part)
                    sums[q] = part if sums[q] is None else sums[q] + part
            if k == count - 1:
                for q in range(4):
                    stats[q] += sums[q]

        return [functools.partial(piece, k) for k in range(count)]

    def step(trip, slot, diag):
        mxu = sim_pieces(trip + 1, slot) + grad_pieces(trip, slot)
        vpu = weight_pieces(trip + slot, 1 - slot, len(mxu), diag)
        for a, b in zip(mxu, vpu):
            a()
            b()

    def take_img(k):
        img(k).wait_recv()
        for kb in range(kblk):
            block = x_all[kb, rows + k * TR:rows + (k + 1) * TR, :].astype(F32).T.astype(BF16)
            for q in range(TR // LANE):
                xt_all[nblk + k * (TR // LANE) + q, kb * LANE:(kb + 1) * LANE, :] = block[:, q * LANE:(q + 1) * LANE]

    def pass_on(k):
        col(k).wait_recv()
        fwd(k).start()

    def add_part(k):
        q_send(k).wait_recv()
        v_all[:, (SEG + k) * TC:(SEG + k) * TC + HALF] += v_part[k % 2]
        if k + 2 < SEG:
            pl.semaphore_signal(free_sem, inc=1, device_id=(core_nbr,), device_id_type=MESH)

    def send_part(k):
        if k >= 2:
            pl.semaphore_wait(free_sem, 1)
        q_send(k).start()

    events = {}

    def at(trip, fn, k):
        events.setdefault(trip, []).append(functools.partial(fn, k))

    for k in range(SEG):
        if k >= 2:
            at((first_use(lambda r, g: g == k) - 2) // 2, lambda k: (load(k).wait(), own(k).wait_recv()), k)
        at(FORWARD_TRIP[k], pass_on, k)
        use = (first_use(lambda r, g: g == SEG + k) - 2) // 2
        assert use > FORWARD_TRIP[k]
        at(use, lambda k: fwd(k).wait_recv(), k)
        at((first_use(lambda r, g: r == SEG + k) - 2) // 2, take_img, k)
        at(last_use(lambda r, g: r == SEG + k) // 2 + 1, lambda k: u_send(k).start(), k)
        done = last_use(lambda r, g: g == SEG + k) // 2 + 1
        at(done, send_part, k)
        at(done + 1, add_part, k)
        at(done + 2, lambda k: v_send(k).start(), k)

    def trips(first, last, diag):
        def body(p, carry):
            for trip in range(first, last):
                if trip in events:
                    @pl.when(p == trip)
                    def _():
                        for fn in events[trip]:
                            fn()
            step(p, 0, diag)
            step(p, 1, diag)
            return carry
        lax.fori_loop(first, last, body, 0)

    load(SEG).wait()
    for k in range(2):
        load(k).wait()
        own(k).wait_recv()
        for piece in sim_pieces(0, k):
            piece()
        if k == 0:
            for piece in weight_pieces(0, 0, 1, True):
                piece()
    load(SEG + 1).wait()
    last = NT // 2 - 1
    trips(0, DIAG_TRIPS, True)
    trips(DIAG_TRIPS, last, False)
    assert max(events) < last
    for piece in grad_pieces(last, 0) + weight_pieces(last, 1, 1, False) + grad_pieces(last, 1):
        piece()
    for k in range(SEG):
        b_send(k).start()
    for k in range(SEG + 1):
        store(k).start()
    for k in range(SEG + 1):
        store(k).wait()
    for k in range(SEG):
        img(k).wait_send()
        own(k).wait_send()
        col(k).wait_send()
        fwd(k).wait_send()
        q_send(k).wait_send()
        for copy in (u_send(k), v_send(k), b_send(k)):
            copy.wait()


def normalize_rows(emb):
    emb32 = emb.astype(F32)
    inv_norm = lax.rsqrt(jnp.sum(emb32 * emb32, axis=-1, keepdims=True))
    return emb32 * inv_norm, inv_norm


def project_back(unit_rows, inv_norm, grad_dir):
    radial = jnp.sum(unit_rows * grad_dir, axis=-1, keepdims=True)
    return (grad_dir - unit_rows * radial) * inv_norm


def lane_blocks(mat):
    return mat.reshape(mat.shape[0], mat.shape[1] // LANE, LANE).transpose(1, 0, 2)


def solution(mesh):
    group_size = mesh.shape['dp']

    def local_fn(img_emb, txt_emb, log_temp, logit_bias):
        rows, dim = img_emb.shape
        total_rows = rows * group_size
        img_unit, img_inv = normalize_rows(img_emb)
        txt_unit, txt_inv = normalize_rows(txt_emb)
        img_b = img_unit.astype(BF16)
        txt_b = txt_unit.astype(BF16)
        temp_scale = jnp.exp(log_temp)
        scal = jnp.stack([temp_scale * LOG2E, logit_bias * LOG2E])
        nblk, kblk = rows // LANE, dim // LANE
        half_out = jax.ShapeDtypeStruct((dim, rows), F32)
        any_spec = pl.BlockSpec(memory_space=pl.ANY)
        dma = pltpu.SemaphoreType.DMA
        u_own, v_own, u_in, v_in, vp_in, stats = pl.pallas_call(
            kernel,
            out_shape=[half_out] * 5 + [jax.ShapeDtypeStruct((4, 8, HC), F32)],
            in_specs=[pl.BlockSpec(memory_space=pltpu.SMEM)] + [any_spec] * 3,
            out_specs=[any_spec] * 5 + [pl.BlockSpec(memory_space=pltpu.VMEM)],
            scratch_shapes=[
                pltpu.VMEM((kblk, 2 * rows, LANE), BF16),
                pltpu.VMEM((2 * nblk, dim, LANE), BF16),
                pltpu.VMEM((4 * nblk, dim, LANE), BF16),
                pltpu.VMEM((dim, 2 * rows), F32),
                pltpu.VMEM((dim, 4 * rows), F32),
                pltpu.VMEM((TR, TC), F32),
                pltpu.VMEM((TR, TC), F32),
                pltpu.VMEM((TC // LANE, TR, LANE), BF16),
                pltpu.VMEM((TC // LANE, TR, LANE), BF16),
                pltpu.VMEM((2, dim, HALF), F32),
                dma((SEG + 2,)),
            ] + [dma((SEG,))] * 16 + [dma((SEG + 1,)), pltpu.SemaphoreType.REGULAR],
            compiler_params=pltpu.CompilerParams(
                collective_id=0, has_side_effects=True, vmem_limit_bytes=67043328),
        )(scal, lane_blocks(img_b), lane_blocks(img_b.T), lane_blocks(txt_b.T))
        sums = lax.psum(jnp.sum(stats, axis=(1, 2)), 'dp') / total_rows
        loss = LN2 * sums[0] + (sums[2] - sums[1])
        grad_img = project_back(img_unit, img_inv, temp_scale * (u_own + u_in).T)
        grad_txt = project_back(txt_unit, txt_inv, temp_scale * ((v_own + vp_in) + v_in).T)
        return loss, grad_img, grad_txt, temp_scale * sums[3], sums[2]

    return jax.shard_map(
        local_fn,
        mesh=mesh,
        in_specs=(P('dp', None), P('dp', None), P(), P()),
        out_specs=(P(), P('dp', None), P('dp', None), P(), P()),
        check_vma=False,
    )
```

time: 860 us -> 312 us (0.36)
  matrix products: 377 us -> 0 us
  waiting for transfers between devices: 339 us -> 0 us
  Pallas kernels: 0 us -> 201 us
  blocking collectives: 76.3 us -> 22.2 us
  local copies, waits for them, and re-layouts: 11.7 us -> 44 us
  other arithmetic: 45.4 us -> 36.7 us
    dot_general x24 -> x0, matrix products: 377 us -> none  [the longest x8 188 us: pair_terms(): jnp.einsum('id,jd->ij', img_b, txt_blk, preferred_element_type=jnp.float32)]
    ppermute x15 -> x0, waiting for transfers between devices: 339 us -> none  [the longest x7 219 us: visit_step(): txt_blk = lax.ppermute(txt_blk, 'dp', shift_pairs)]
    pallas_call x0 -> x1, Pallas kernels: none -> 201 us  [local_fn(): pl.pallas_call(kernel, out_shape=[half_out] * 5 + [jax.ShapeDtypeStruct((...]
    psum x1, blocking collectives: 76.3 us -> 22.2 us  [local_fn(): sums = lax.psum(jnp.sum(stats, axis=(1, 2)), 'dp') / total_rows]
    unnamed x20, local copies, waits for them, and re-layouts: 0.05 us -> 21.5 us
    add x7 -> x0, other arithmetic: 19.8 us -> none  [visit_step(): stat_sums + new_sums]
    reshape x0 -> x3, local copies, waits for them, and re-layouts: none -> 13.2 us  [lane_blocks(): mat.reshape(mat.shape[0], mat.shape[1] // LANE, LANE).transpose(1, 0, 2)]
    while x49 -> x0, local copies, waits for them, and re-layouts: 11 us -> none
  transfers between devices with their start and end apart: 15 -> 0, of which waited for: 14 -> 0; matrix products, arithmetic and copies ran while one was open for 33% -> 0% of each run, Pallas kernels for 0% -> 0%
where the time goes in v1:
time: 312 us; the launch traced here: 311 us
  Pallas kernels  201 us (64%)
  local copies, waits for them, and re-layouts  44 us (14%)
  other arithmetic  36.7 us (12%)
  blocking collectives  22.2 us (7%)
  between operations  6.93 us (2%)
    pallas_call x1, Pallas kernels, local_fn(): pl.pallas_call(kernel, out_shape=[half_out] * 5 + [jax.ShapeDtypeStruct((...  201 us
    psum x1, blocking collectives, local_fn(): sums = lax.psum(jnp.sum(stats, axis=(1, 2)), 'dp') / total_rows  22.2 us
    unnamed x20, local copies, waits for them, and re-layouts  21.5 us
    reduce_sum x2, other arithmetic, project_back(): radial = jnp.sum(unit_rows * grad_dir, axis=-1, keepdims=True)  18.1 us
    reshape x3, local copies, waits for them, and re-layouts, lane_blocks(): mat.reshape(mat.shape[0], mat.shape[1] // LANE, LANE).transpose(1, 0, 2)  13.2 us
    transpose x2, local copies, waits for them, and re-layouts, local_fn(): u_own, v_own, u_in, v_in, vp_in, stats = pl.pallas_call(kernel, out_shape...  8.75 us

profile of v1, /device:TPU:0, one launch (start us, length us, event | category | flops | bytes accessed | tf_op | source)
XLA Modules:
  0.0 311.3 jit_solution(9023230076046246700)
XLA Ops:
  2.0 0.6 pad_maximum_fusion.scal
  2.6 3.0 copy.13
  5.5 0.0 copy-start
  5.6 0.6 fusion.9
  6.1 4.8 %copy.17 = bf16[2048,640]{0,1:T(8,128)(2,1)} copy(bf16[2048,640]{1,0:T(8,128)(2,1)} %param.5) | data formatting | bytes 5242880 | tf_op args[1]
  10.9 2.3 fusion.13
  13.3 0.6 copy-done.6
  13.8 4.0 %fusion.14 = bf16[640,2048]{1,0:T(8,128)(2,1)} fusion(bf16[2048,640]{0,1:T(8,128)(2,1)} %copy.17, f32[2048]{0:T(1024)S(1)} %rsqrt.17), kind=kLoop, calls=%fused_computation.20 | loop fusion | flops 3932160 | bytes 5251072 | tf_op jit(solution)/shard_map/transpose | solution.py:346
  17.8 4.4 %copy.18 = bf16[640,2048]{0,1:T(8,128)(2,1)} copy(bf16[640,2048]{1,0:T(8,128)(2,1)} %fusion.14) | data formatting | bytes 5242880 | tf_op jit(solution)/shard_map/transpose | solution.py:346
  22.2 4.4 %copy.19 = bf16[640,16,128]{2,0,1:T(8,128)(2,1)} copy(bf16[640,16,128]{0,2,1:T(8,128)(2,1)} %bitcast.25) | data formatting | bytes 5242880 | tf_op jit(solution)/shard_map/reshape | solution.py:307
  26.6 2.1 fusion.16
  28.7 4.4 %copy.15 = bf16[640,2048]{0,1:T(8,128)(2,1)} copy(bf16[640,2048]{1,0:T(8,128)(2,1)} %fusion.16) | data formatting | bytes 5242880 | tf_op jit(solution)/shard_map/transpose | solution.py:346
  33.1 4.4 %copy.16 = bf16[640,16,128]{2,0,1:T(8,128)(2,1)} copy(bf16[640,16,128]{0,2,1:T(8,128)(2,1)} %bitcast.26) | data formatting | bytes 5242880 | tf_op jit(solution)/shard_map/reshape | solution.py:307
  37.5 0.0 copy-done
  37.5 0.0 copy-done.4
  37.5 2.1 fusion.5
  39.6 4.4 %copy.14 = bf16[2048,5,128]{2,0,1:T(8,128)(2,1)} copy(bf16[2048,5,128]{0,2,1:T(8,128)(2,1)} %bitcast.27) | data formatting | bytes 5242880 | tf_op jit(solution)/shard_map/reshape | solution.py:307
  44.0 201.4 %shard_map.83 = (f32[640,2048]{1,0:T(8,128)}, f32[640,2048]{1,0:T(8,128)}, f32[640,2048]{1,0:T(8,128)}, f32[640,2048]{1,0:T(8,128)}, f32[640,2048]{1,0:T(8,128)}, /*index=5*/f32[4,8,256]{2,1,0:T(8,128)}) custom-call(f32[2]{0:T(128)} %pad_maximum_fusion.scal, bf16[5,2048,128]{2,1,0:T(8,128)(2,1)} %bitcast.24, bf16[16,640,128]{2,1,0:T(8,128)(2,1)} %bitcast.23, ...), custom_call_target="tpu_custom_call" | custom-call | tf_op jit(solution)/shard_map/pallas_call | solution.py:326
  245.4 0.9 reduce_sum.47
  246.3 22.2 %psum.7 = f32[4]{0:T(128)S(1)} all-reduce(f32[4]{0:T(128)S(1)} %reduce_sum.47), channel_id=1, replica_groups=mesh['dp'=8] {'dp'}, use_global_device_ids=true, to_apply=%region_3.0 | all-reduce | flops 4 | bytes 32 | tf_op jit(solution)/shard_map/psum | solution.py:347
  268.5 0.6 fusion.15
  271.7 0.0 copy-start.1
  271.7 0.0 copy-start.2
  271.7 0.0 copy-start.3
  271.8 6.5 %fusion.6 = f32[2048]{0:T(1024)S(1)} fusion(bf16[2048,640]{0,1:T(8,128)(2,1)} %copy-done, f32[2048]{0:T(1024)} %copy-done.4, f32[640,2048]{1,0:T(8,128)} %get-tuple-element.12, f32[640,2048]{1,0:T(8,128)} %get-tuple-element.13, f32[]{:T(128)S(6)} %exp.3), kind=kLoop, calls=%fused_computation.10 | loop fusion | flops 7862272 | bytes 13123588 | tf_op jit(solution)/shard_map/reduce_sum | solution.py:302
  278.2 0.0 copy-done.1
  278.2 0.0 copy-done.2
  278.2 1.3 copy-done.3
  279.6 11.6 %fusion.10 = (f32[2048]{0:T(1024)S(1)}, f32[640,2048]{1,0:T(8,128)}, f32[2048,640]{0,1:T(8,128)}) fusion(bf16[2048,640]{0,1:T(8,128)(2,1)S(1)} %copy-done.2, f32[2048]{0:T(1024)S(1)} %copy-done.7, f32[640,2048]{1,0:T(8,128)} %get-tuple-element.16, f32[640,2048]{1,0:T(8,128)} %get-tuple-element.14, f32[640,2048]{1,0:T(8,128)} %get-tuple-element.15, ...), kind=kLoop, calls=%fused_computation.14 | loop fusion | flops 18348032 | bytes 41975812 | tf_op jit(solution)/shard_map/reduce_sum | solution.py:302
  291.2 6.1 %fusion.12 = f32[2048,640]{0,1:T(8,128)} fusion(bf16[2048,640]{0,1:T(8,128)(2,1)S(1)} %copy-done.2, f32[640,2048]{1,0:T(8,128)} %get-tuple-element.28, f32[2048]{0:T(1024)S(1)} %get-tuple-element.27, f32[2048]{0:T(1024)S(1)} %copy-done.7), kind=kLoop, calls=%fused_computation.16 | loop fusion | flops 6553600 | bytes 13123584 | tf_op jit(solution)/shard_map/mul | solution.py:303
  297.3 5.9 %copy.21 = f32[2048,640]{1,0:T(8,128)} copy(f32[2048,640]{0,1:T(8,128)} %fusion.12) | data formatting | bytes 10485760
  303.2 5.9 %copy.20 = f32[2048,640]{1,0:T(8,128)} copy(f32[2048,640]{0,1:T(8,128)} %get-tuple-element.33) | data formatting | bytes 10485760
  (9 shorter events, 0.0 us)
Async XLA Ops:
  5.5 31.9 %copy-start = (bf16[2048,640]{0,1:T(8,128)(2,1)}, bf16[2048,640]{0,1:T(8,128)(2,1)S(1)}, u32[]{:S(2)}) copy-start(bf16[2048,640]{0,1:T(8,128)(2,1)S(1)} %copy.13) | copy-start | bytes 7864324
  6.1 31.4 %copy-start.4 = (f32[2048]{0:T(1024)}, f32[2048]{0:T(1024)S(1)}, u32[]{:S(2)}) copy-start(f32[2048]{0:T(1024)S(1)} %rsqrt.16) | copy-start | bytes 24580
  13.2 0.6 copy-start.6
  271.7 6.5 %copy-start.1 = (bf16[2048,640]{0,1:T(8,128)(2,1)S(1)}, bf16[2048,640]{0,1:T(8,128)(2,1)}, u32[]{:S(2)}) copy-start(bf16[2048,640]{0,1:T(8,128)(2,1)} %copy-done) | copy-start | bytes 7864324
  271.7 6.5 %copy-start.2 = (bf16[2048,640]{0,1:T(8,128)(2,1)S(1)}, bf16[2048,640]{0,1:T(8,128)(2,1)}, u32[]{:S(2)}) copy-start(bf16[2048,640]{0,1:T(8,128)(2,1)} %copy.17) | copy-start | bytes 7864324
  271.7 7.8 %copy-start.3 = (f32[640,2048]{1,0:T(8,128)S(1)}, f32[640,2048]{1,0:T(8,128)}, u32[]{:S(2)}) copy-start(f32[640,2048]{1,0:T(8,128)} %get-tuple-element.12) | copy-start | bytes 15728644
  271.7 7.8 %copy-start.5 = (f32[2048]{0:T(1024)S(1)}, f32[2048]{0:T(1024)}, u32[]{:S(2)}) copy-start(f32[2048]{0:T(1024)} %copy-done.4) | copy-start | bytes 24580
  271.8 7.8 %copy-start.7 = (f32[2048]{0:T(1024)S(1)}, f32[2048]{0:T(1024)}, u32[]{:S(2)}) copy-start(f32[2048]{0:T(1024)} %copy-done.6) | copy-start | bytes 24580

commit v2 on v1

--- a/solution.py
+++ b/solution.py
@@ -50,16 +50,16 @@
     return min(t for t, rg in enumerate(ORDER) if match(*rg))
 
 
-def kernel(scal, x_hbm, xt_hbm, yt_hbm, u_out, v_out, u_in, v_in, vp_in, stats, x_all, xt_all, yt_all, u_all, v_all,
-           s0, s1, h0, h1, v_part, loc_sem, img_s, img_r, own_s, own_r, col_s, col_r, fwd_s, fwd_r, u_s, u_r,
-           q_s, q_r, v_s, v_r, b_s, b_r, out_sem, free_sem):
+def kernel(scal, img_hbm, txt_hbm, u_out, v_out, u_in, v_in, vp_in, sums_out, stats, st_buf, st_in, x_all, xt_all, yt_all, u_all, v_all,
+           s0, s1, h0, h1, v_part, x_sem, y_sem, img_s, img_r, own_s, own_r, col_s, col_r, fwd_s, fwd_r, u_s, u_r,
+           q_s, q_r, v_s, v_r, b_s, b_r, out_sem, st_s, st_r, free_sem):
     me = lax.axis_index('dp')
     core_nbr, row_nbr, col_nbr = me ^ 1, me ^ 2, me ^ 4
     dim = u_all.shape[0]
-    rows = x_hbm.shape[1]
+    rows = img_hbm.shape[0]
     nblk = rows // LANE
     cblk = HALF // LANE
-    kblk = x_hbm.shape[0]
+    kblk = dim // LANE
 
     barrier = pltpu.get_barrier_semaphore()
     for nbr in (core_nbr, row_nbr, col_nbr):
@@ -70,14 +70,14 @@
                                             device_id=(dev,), device_id_type=MESH)
 
     def img(k):
-        return remote(x_hbm.at[:, pl.ds(k * TR, TR)], x_all.at[:, pl.ds(rows + k * TR, TR)], img_s, img_r, k, row_nbr)
+        return remote(x_all.at[:, pl.ds(k * TR, TR)], x_all.at[:, pl.ds(rows + k * TR, TR)], img_s, img_r, k, row_nbr)
 
     def own(k):
-        return remote(yt_hbm.at[pl.ds(k * cblk, cblk)], yt_all.at[pl.ds(k * 2 * cblk + cblk, cblk)], own_s, own_r, k,
+        return remote(yt_all.at[pl.ds(k * 2 * cblk, cblk)], yt_all.at[pl.ds(k * 2 * cblk + cblk, cblk)], own_s, own_r, k,
                       core_nbr)
 
     def col(k):
-        return remote(yt_hbm.at[pl.ds(k * cblk, cblk)], yt_all.at[pl.ds((SEG + k) * 2 * cblk, cblk)], col_s, col_r, k,
+        return remote(yt_all.at[pl.ds(k * 2 * cblk, cblk)], yt_all.at[pl.ds((SEG + k) * 2 * cblk, cblk)], col_s, col_r, k,
                       col_nbr)
 
     def fwd(k):
@@ -96,13 +96,20 @@
     def b_send(k):
         return remote(v_all.at[:, pl.ds(k * TC + HALF, HALF)], vp_in.at[:, pl.ds(k * HALF, HALF)], b_s, b_r, k, core_nbr)
 
-    def load(k):
-        if k < SEG:
-            return pltpu.make_async_copy(yt_hbm.at[pl.ds(k * cblk, cblk)], yt_all.at[pl.ds(k * 2 * cblk, cblk)],
-                                         loc_sem.at[k])
-        if k == SEG:
-            return pltpu.make_async_copy(x_hbm, x_all.at[:, pl.ds(0, rows)], loc_sem.at[k])
-        return pltpu.make_async_copy(xt_hbm, xt_all.at[pl.ds(0, nblk)], loc_sem.at[k])
+    def load_img(kb):
+        return pltpu.make_async_copy(img_hbm.at[:, pl.ds(kb * LANE, LANE)], x_all.at[kb, pl.ds(0, rows)], x_sem.at[kb])
+
+    def load_txt(k, kb):
+        return pltpu.make_async_copy(txt_hbm.at[pl.ds(k * TR, TR), pl.ds(kb * LANE, LANE)],
+                                     wgt[k % 2].at[kb], y_sem.at[k * kblk + kb])
+
+    def swap(k, value):
+        nbr = (core_nbr, row_nbr, col_nbr)[k]
+        st_buf[k] = value
+        copy = remote(st_buf.at[k], st_in.at[k], st_s, st_r, k, nbr)
+        copy.start()
+        copy.wait()
+        return st_buf[k] + st_in[k]
 
     def store(k):
         if k < SEG:
@@ -110,19 +117,50 @@
                                          out_sem.at[k])
         return pltpu.make_async_copy(u_all.at[:, pl.ds(0, rows)], u_out, out_sem.at[k])
 
-    for k in (SEG, 0, 1, 2, 3, SEG + 1):
-        load(k).start()
-    pl.semaphore_wait(barrier, 3)
+    sim, wgt = (s0, s1), (h0, h1)
+    for kb in range(kblk):
+        load_txt(0, kb).start()
+    for kb in range(kblk):
+        load_img(kb).start()
+    for kb in range(kblk):
+        load_txt(1, kb).start()
+
+    def unit(blocks):
+        wide = [block.astype(F32) for block in blocks]
+        norm2 = jnp.sum(functools.reduce(jnp.add, [w * w for w in wide]), axis=-1, keepdims=True)
+        inv_norm = lax.rsqrt(norm2)
+        return [(w * inv_norm).astype(BF16) for w in wide]
+
+    def put_transposed(ref, first, kb, block):
+        flipped = block.T
+        for q in range(TR // LANE):
+            ref[first + q, kb * LANE:(kb + 1) * LANE, :] = flipped[:, q * LANE:(q + 1) * LANE]
+
     for k in range(SEG):
+        for kb in range(kblk):
+            load_txt(k, kb).wait()
+        for kb, block in enumerate(unit([wgt[k % 2][kb] for kb in range(kblk)])):
+            put_transposed(yt_all, k * 2 * cblk, kb, block)
+        if k == 0:
+            for kb in range(kblk):
+                load_img(kb).wait()
+        if k + 2 < SEG:
+            for kb in range(kblk):
+                load_txt(k + 2, kb).start()
+        at_rows = slice(k * TR, (k + 1) * TR)
+        for kb, block in enumerate(unit([x_all[kb, at_rows, :] for kb in range(kblk)])):
+            x_all[kb, at_rows, :] = block
+            put_transposed(xt_all, k * (TR // LANE), kb, block)
+        if k == 0:
+            pl.semaphore_wait(barrier, 3)
+        col(k).start()
+        img(k).start()
         own(k).start()
-        img(k).start()
-        col(k).start()
 
     scale2, bias2 = scal[0], scal[1]
     stats[...] = jnp.zeros_like(stats)
     u_all[...] = jnp.zeros_like(u_all)
     v_all[...] = jnp.zeros_like(v_all)
-    sim, wgt = (s0, s1), (h0, h1)
 
     def cat(ref, first, count, rows_at):
         return jnp.concatenate([ref[first + q, rows_at, :] for q in range(count)], axis=1)
@@ -209,9 +247,7 @@
     def take_img(k):
         img(k).wait_recv()
         for kb in range(kblk):
-            block = x_all[kb, rows + k * TR:rows + (k + 1) * TR, :].astype(F32).T.astype(BF16)
-            for q in range(TR // LANE):
-                xt_all[nblk + k * (TR // LANE) + q, kb * LANE:(kb + 1) * LANE, :] = block[:, q * LANE:(q + 1) * LANE]
+            put_transposed(xt_all, nblk + k * (TR // LANE), kb, x_all[kb, rows + k * TR:rows + (k + 1) * TR, :])
 
     def pass_on(k):
         col(k).wait_recv()
@@ -235,7 +271,7 @@
 
     for k in range(SEG):
         if k >= 2:
-            at((first_use(lambda r, g: g == k) - 2) // 2, lambda k: (load(k).wait(), own(k).wait_recv()), k)
+            at((first_use(lambda r, g: g == k) - 2) // 2, lambda k: own(k).wait_recv(), k)
         at(FORWARD_TRIP[k], pass_on, k)
         use = (first_use(lambda r, g: g == SEG + k) - 2) // 2
         assert use > FORWARD_TRIP[k]
@@ -260,16 +296,13 @@
             return carry
         lax.fori_loop(first, last, body, 0)
 
-    load(SEG).wait()
     for k in range(2):
-        load(k).wait()
         own(k).wait_recv()
         for piece in sim_pieces(0, k):
             piece()
         if k == 0:
             for piece in weight_pieces(0, 0, 1, True):
                 piece()
-    load(SEG + 1).wait()
     last = NT // 2 - 1
     trips(0, DIAG_TRIPS, True)
     trips(DIAG_TRIPS, last, False)
@@ -280,6 +313,13 @@
         b_send(k).start()
     for k in range(SEG + 1):
         store(k).start()
+    total = stats[:, :, :LANE]
+    for c in range(LANE, HC, LANE):
+        total += stats[:, :, c:c + LANE]
+    for k in range(3):
+        total = swap(k, total)
+    for q in range(4):
+        sums_out[q] = jnp.sum(total[q])
     for k in range(SEG + 1):
         store(k).wait()
     for k in range(SEG):
@@ -292,19 +332,17 @@
             copy.wait()
 
 
-def normalize_rows(emb):
-    emb32 = emb.astype(F32)
-    inv_norm = lax.rsqrt(jnp.sum(emb32 * emb32, axis=-1, keepdims=True))
-    return emb32 * inv_norm, inv_norm
-
-
-def project_back(unit_rows, inv_norm, grad_dir):
-    radial = jnp.sum(unit_rows * grad_dir, axis=-1, keepdims=True)
-    return (grad_dir - unit_rows * radial) * inv_norm
-
-
-def lane_blocks(mat):
-    return mat.reshape(mat.shape[0], mat.shape[1] // LANE, LANE).transpose(1, 0, 2)
+def finish(temp, img, txt, u_own, u_in, v_own, vp_in, v_in, img_out, txt_out):
+    def project(emb, total, out):
+        emb32 = emb[...].astype(F32)
+        inv_norm = lax.rsqrt(jnp.sum(emb32 * emb32, axis=-1, keepdims=True))
+        unit_rows = emb32 * inv_norm
+        grad_dir = (total * temp[0]).T
+        radial = jnp.sum(unit_rows * grad_dir, axis=-1, keepdims=True)
+        out[...] = (grad_dir - unit_rows * radial) * inv_norm
+
+    project(img, u_own[...] + u_in[...], img_out)
+    project(txt, (v_own[...] + vp_in[...]) + v_in[...], txt_out)
 
 
 def solution(mesh):
@@ -313,22 +351,22 @@
     def local_fn(img_emb, txt_emb, log_temp, logit_bias):
         rows, dim = img_emb.shape
         total_rows = rows * group_size
-        img_unit, img_inv = normalize_rows(img_emb)
-        txt_unit, txt_inv = normalize_rows(txt_emb)
-        img_b = img_unit.astype(BF16)
-        txt_b = txt_unit.astype(BF16)
         temp_scale = jnp.exp(log_temp)
         scal = jnp.stack([temp_scale * LOG2E, logit_bias * LOG2E])
         nblk, kblk = rows // LANE, dim // LANE
         half_out = jax.ShapeDtypeStruct((dim, rows), F32)
         any_spec = pl.BlockSpec(memory_space=pl.ANY)
+        smem_spec = pl.BlockSpec(memory_space=pltpu.SMEM)
         dma = pltpu.SemaphoreType.DMA
-        u_own, v_own, u_in, v_in, vp_in, stats = pl.pallas_call(
+        u_own, v_own, u_in, v_in, vp_in, sums = pl.pallas_call(
             kernel,
-            out_shape=[half_out] * 5 + [jax.ShapeDtypeStruct((4, 8, HC), F32)],
-            in_specs=[pl.BlockSpec(memory_space=pltpu.SMEM)] + [any_spec] * 3,
-            out_specs=[any_spec] * 5 + [pl.BlockSpec(memory_space=pltpu.VMEM)],
+            out_shape=[half_out] * 5 + [jax.ShapeDtypeStruct((4,), F32)],
+            in_specs=[smem_spec] + [any_spec] * 2,
+            out_specs=[any_spec] * 5 + [smem_spec],
             scratch_shapes=[
+                pltpu.VMEM((4, 8, HC), F32),
+                pltpu.VMEM((3, 4, 8, LANE), F32),
+                pltpu.VMEM((3, 4, 8, LANE), F32),
                 pltpu.VMEM((kblk, 2 * rows, LANE), BF16),
                 pltpu.VMEM((2 * nblk, dim, LANE), BF16),
                 pltpu.VMEM((4 * nblk, dim, LANE), BF16),
@@ -339,15 +377,24 @@
                 pltpu.VMEM((TC // LANE, TR, LANE), BF16),
                 pltpu.VMEM((TC // LANE, TR, LANE), BF16),
                 pltpu.VMEM((2, dim, HALF), F32),
-                dma((SEG + 2,)),
-            ] + [dma((SEG,))] * 16 + [dma((SEG + 1,)), pltpu.SemaphoreType.REGULAR],
+                dma((kblk,)),
+                dma((SEG * kblk,)),
+            ] + [dma((SEG,))] * 16 + [dma((SEG + 1,)), dma((3,)), dma((3,)), pltpu.SemaphoreType.REGULAR],
             compiler_params=pltpu.CompilerParams(
                 collective_id=0, has_side_effects=True, vmem_limit_bytes=67043328),
-        )(scal, lane_blocks(img_b), lane_blocks(img_b.T), lane_blocks(txt_b.T))
-        sums = lax.psum(jnp.sum(stats, axis=(1, 2)), 'dp') / total_rows
+        )(scal, img_emb, txt_emb)
+        sums = sums / total_rows
         loss = LN2 * sums[0] + (sums[2] - sums[1])
-        grad_img = project_back(img_unit, img_inv, temp_scale * (u_own + u_in).T)
-        grad_txt = project_back(txt_unit, txt_inv, temp_scale * ((v_own + vp_in) + v_in).T)
+        step_rows = 256
+        emb_spec = pl.BlockSpec((step_rows, dim), lambda i: (i, 0))
+        col_spec = pl.BlockSpec((dim, step_rows), lambda i: (0, i))
+        grad_img, grad_txt = pl.pallas_call(
+            finish,
+            grid=(rows // step_rows,),
+            out_shape=[jax.ShapeDtypeStruct((rows, dim), F32)] * 2,
+            in_specs=[smem_spec] + [emb_spec] * 2 + [col_spec] * 5,
+            out_specs=[emb_spec] * 2,
+        )(temp_scale[None], img_emb, txt_emb, u_own, u_in, v_own, vp_in, v_in)
         return loss, grad_img, grad_txt, temp_scale * sums[3], sums[2]
 
     return jax.shard_map(

time: 312 us -> 230 us (0.74)
  local copies, waits for them, and re-layouts: 44 us -> 0.6 us
  other arithmetic: 36.7 us -> 0.59 us
  blocking collectives: 22.2 us -> 0 us
  Pallas kernels: 201 us -> 222 us
    psum x1 -> x0, blocking collectives: 22.2 us -> none  [local_fn(): sums = lax.psum(jnp.sum(stats, axis=(1, 2)), 'dp') / total_rows]
    reduce_sum x5 -> x0, other arithmetic: 21.8 us -> none  [the longest x2 18.1 us: project_back(): radial = jnp.sum(unit_rows * grad_dir, axis=-1, keepdims=True)]
    unnamed x20 -> x2, local copies, waits for them, and re-layouts: 21.5 us -> 0.01 us
    pallas_call x0 -> x1, Pallas kernels: none -> 16.3 us  [local_fn(): pl.pallas_call(finish, grid=(rows // step_rows,), out_shape=[jax.ShapeDty...]
    reshape x3 -> x0, local copies, waits for them, and re-layouts: 13.2 us -> none  [lane_blocks(): mat.reshape(mat.shape[0], mat.shape[1] // LANE, LANE).transpose(1, 0, 2)]
    transpose x2 -> x0, local copies, waits for them, and re-layouts: 8.75 us -> none  [local_fn(): u_own, v_own, u_in, v_in, vp_in, stats = pl.pallas_call(kernel, out_shape...]
    mul x1 -> x0, other arithmetic: 6.14 us -> none  [project_back(): return (grad_dir - unit_rows * radial) * inv_norm]
    transpose x2 -> x0, other arithmetic: 6.09 us -> none  [local_fn(): u_own, v_own, u_in, v_in, vp_in, stats = pl.pallas_call(kernel, out_shape...]
where the time goes in v2:
time: 230 us
  Pallas kernels  222 us (97%)
  between operations  6.8 us (3%)
    pallas_call x1, Pallas kernels, local_fn(): pl.pallas_call(kernel, out_shape=[half_out] * 5 + [jax.ShapeDtypeStruct((...  205 us
    pallas_call x1, Pallas kernels, local_fn(): pl.pallas_call(finish, grid=(rows // step_rows,), out_shape=[jax.ShapeDty...  16.3 us

profile of v2, /device:TPU:0, one launch (start us, length us, event | category | flops | bytes accessed | tf_op | source)
XLA Modules:
  0.0 229.6 jit_solution(13073118333393601082)
XLA Ops:
  2.0 0.6 pad_maximum_fusion.scal
  2.5 205.3 %shard_map.83 = (f32[640,2048]{1,0:T(8,128)}, f32[640,2048]{1,0:T(8,128)}, f32[640,2048]{1,0:T(8,128)}, f32[640,2048]{1,0:T(8,128)}, f32[640,2048]{1,0:T(8,128)}, /*index=5*/f32[4]{0:T(128)}) custom-call(f32[2]{0:T(128)} %pad_maximum_fusion.scal, bf16[2048,640]{1,0:T(8,128)(2,1)} %img.1, bf16[2048,640]{1,0:T(8,128)(2,1)} %txt.1), custom_call_target="tpu_custom_call" | custom-call | tf_op jit(solution)/shard_map/pallas_call | solution.py:361
  207.9 0.0 copy-start
  207.9 16.3 %shard_map.84 = (f32[2048,640]{1,0:T(8,128)}, f32[2048,640]{1,0:T(8,128)}) custom-call(f32[1]{0:T(128)} %bitcast.5.temp, bf16[2048,640]{1,0:T(8,128)(2,1)} %img.1, bf16[2048,640]{1,0:T(8,128)(2,1)} %txt.1, f32[640,2048]{1,0:T(8,128)} %get-tuple-element.14.u_own, f32[640,2048]{1,0:T(8,128)} %get-tuple-element.15.u_in, f32[640,2048]{1,0:T(8,128)} %get-tuple-element.16.v_own, ...), custom_call_target="tpu_custom_call" | custom-call | tf_op jit(solution)/shard_map/pallas_call | solution.py:391
  224.2 0.0 copy-done
  224.2 0.6 fusion
  (1 shorter events, 0.0 us)
Async XLA Ops:
  207.9 16.3 %copy-start = (f32[4]{0:T(128)S(1)}, f32[4]{0:T(128)}, u32[]{:S(2)}) copy-start(f32[4]{0:T(128)} %get-tuple-element.13) | copy-start | bytes 52

commit v3 on v2

--- a/solution.py
+++ b/solution.py
@@ -18,28 +18,29 @@
 SEG = 4
 
 ORDER = [
-    (0, 0), (1, 1), (2, 2), (3, 3), (0, 1), (1, 0), (0, 2), (2, 0),
-    (4, 0), (4, 1), (0, 4), (1, 4), (2, 4), (3, 4), (4, 4), (4, 2),
-    (4, 3), (4, 5), (5, 4), (5, 0), (6, 4), (5, 1), (4, 6), (5, 2),
-    (7, 4), (5, 3), (4, 7), (5, 5), (5, 6), (5, 7), (0, 5), (1, 5),
-    (2, 5), (3, 5), (6, 5), (7, 5), (6, 0), (6, 1), (6, 2), (6, 3),
-    (6, 6), (6, 7), (0, 6), (1, 6), (2, 6), (3, 6), (7, 6), (7, 7),
-    (7, 0), (7, 1), (7, 2), (7, 3), (0, 7), (1, 7), (2, 7), (3, 7),
-    (0, 3), (3, 0), (1, 2), (2, 1), (1, 3), (3, 1), (2, 3), (3, 2),
+    (0, 0), (1, 1), (2, 2), (3, 3), (0, 1), (1, 0), (4, 0), (4, 1),
+    (4, 2), (4, 3), (0, 4), (1, 4), (2, 4), (3, 4), (4, 4), (5, 4),
+    (4, 5), (6, 4), (4, 6), (5, 0), (5, 1), (5, 5), (7, 4), (5, 6),
+    (4, 7), (5, 2), (5, 3), (5, 7), (0, 5), (1, 5), (2, 5), (3, 5),
+    (6, 5), (7, 5), (6, 0), (6, 1), (6, 2), (6, 3), (6, 6), (6, 7),
+    (0, 6), (1, 6), (2, 6), (3, 6), (7, 6), (7, 7), (7, 0), (7, 1),
+    (7, 2), (7, 3), (0, 7), (1, 7), (2, 7), (3, 7), (2, 0), (3, 0),
+    (2, 1), (3, 1), (0, 2), (1, 2), (3, 2), (0, 3), (1, 3), (2, 3),
 ]
+assert len(set(ORDER)) == 64
 NT = len(ORDER)
 DIAG_TRIPS = 2
-FORWARD_TRIP = (3, 6, 9, 11)
-
-
-def tile_at(trip, parity):
+FORWARD_TRIP = (2, 6, 7, 10)
+
+
+def code_at(trip, parity):
+    codes = [8 * r + g for r, g in ORDER[parity::2]]
     if isinstance(trip, int):
-        return ORDER[2 * trip + parity]
-    code = jnp.int32(8 * ORDER[parity][0] + ORDER[parity][1])
-    for k in range(1, NT // 2):
-        r, g = ORDER[2 * k + parity]
-        code = jnp.where(trip == k, 8 * r + g, code)
-    return code // 8, code % 8
+        return codes[trip]
+    code = jnp.int32(codes[0])
+    for k, value in enumerate(codes[1:], 1):
+        code = jnp.where(trip == k, value, code)
+    return code
 
 
 def last_use(match):
@@ -52,7 +53,7 @@
 
 def kernel(scal, img_hbm, txt_hbm, u_out, v_out, u_in, v_in, vp_in, sums_out, stats, st_buf, st_in, x_all, xt_all, yt_all, u_all, v_all,
            s0, s1, h0, h1, v_part, x_sem, y_sem, img_s, img_r, own_s, own_r, col_s, col_r, fwd_s, fwd_r, u_s, u_r,
-           q_s, q_r, v_s, v_r, b_s, b_r, out_sem, st_s, st_r, free_sem):
+           q_s, q_r, v_s, v_r, b_s, b_r, out_sem, st_s, st_r, in_sem, free_sem):
     me = lax.axis_index('dp')
     core_nbr, row_nbr, col_nbr = me ^ 1, me ^ 2, me ^ 4
     dim = u_all.shape[0]
@@ -111,6 +112,21 @@
         copy.wait()
         return st_buf[k] + st_in[k]
 
+    def load_img(kb):
+        return pltpu.make_async_copy(img_hbm.at[:, pl.ds(kb * LANE, LANE)], x_all.at[kb, pl.ds(0, rows)], x_sem.at[kb])
+
+    def load_txt(k, kb):
+        return pltpu.make_async_copy(txt_hbm.at[pl.ds(k * TR, TR), pl.ds(kb * LANE, LANE)],
+                                     wgt[k % 2].at[kb], y_sem.at[k * kblk + kb])
+
+    def swap(k, value):
+        nbr = (core_nbr, row_nbr, col_nbr)[k]
+        st_buf[k] = value
+        copy = remote(st_buf.at[k], st_in.at[k], st_s, st_r, k, nbr)
+        copy.start()
+        copy.wait()
+        return st_buf[k] + st_in[k]
+
     def store(k):
         if k < SEG:
             return pltpu.make_async_copy(v_all.at[:, pl.ds(k * TC, HALF)], v_out.at[:, pl.ds(k * HALF, HALF)],
@@ -124,6 +140,8 @@
         load_img(kb).start()
     for kb in range(kblk):
         load_txt(1, kb).start()
+
+    u_all[...] = jnp.zeros_like(u_all)
 
     def unit(blocks):
         wide = [block.astype(F32) for block in blocks]
@@ -159,7 +177,6 @@
 
     scale2, bias2 = scal[0], scal[1]
     stats[...] = jnp.zeros_like(stats)
-    u_all[...] = jnp.zeros_like(u_all)
     v_all[...] = jnp.zeros_like(v_all)
 
     def cat(ref, first, count, rows_at):
@@ -170,8 +187,8 @@
 
     every = pl.ds(0, dim)
 
-    def sim_pieces(trip, slot):
-        r, g = tile_at(trip, slot)
+    def sim_pieces(code, slot):
+        r, g = code // 8, code % 8
 
         def piece(k):
             texts = cat(yt_all, g * 2 * cblk + k * cblk, cblk, every)
@@ -180,8 +197,8 @@
 
         return [functools.partial(piece, k) for k in range(2)]
 
-    def grad_pieces(trip, slot):
-        r, g = tile_at(trip, slot)
+    def grad_pieces(code, slot):
+        r, g = code // 8, code % 8
 
         def img_piece():
             u_all[:, aligned(r * TR, TR)] += lax.dot_general(
@@ -195,12 +212,12 @@
 
         return [img_piece] + [functools.partial(txt_piece, k) for k in range(2)]
 
-    def weight_pieces(trip, slot, count, diag):
+    def weight_pieces(code, slot, count, diag):
         blocks = [(r, c) for r in range(0, TR, HR) for c in range(0, TC, HC)]
         per = -(-len(blocks) // count)
         sums = [None] * 4
         if diag:
-            tr, tg = tile_at(trip, slot)
+            tr, tg = code // 8, code % 8
             offset = jnp.where(tr == tg, 0, 4 * TC)
             lag = lax.broadcasted_iota(jnp.int32, (HR, HC), 1) - lax.broadcasted_iota(jnp.int32, (HR, HC), 0)
 
@@ -237,9 +254,9 @@
 
         return [functools.partial(piece, k) for k in range(count)]
 
-    def step(trip, slot, diag):
-        mxu = sim_pieces(trip + 1, slot) + grad_pieces(trip, slot)
-        vpu = weight_pieces(trip + slot, 1 - slot, len(mxu), diag)
+    def step(now, later, slot, diag):
+        mxu = sim_pieces(later[slot], slot) + grad_pieces(now[slot], slot)
+        vpu = weight_pieces((now[1], later[0])[slot], 1 - slot, len(mxu), diag)
         for a, b in zip(mxu, vpu):
             a()
             b()
@@ -277,51 +294,97 @@
         assert use > FORWARD_TRIP[k]
         at(use, lambda k: fwd(k).wait_recv(), k)
         at((first_use(lambda r, g: r == SEG + k) - 2) // 2, take_img, k)
+        at(last_use(lambda r, g: g == k) // 2 + 1, lambda k: b_send(k).start(), k)
+    for k in range(SEG):
         at(last_use(lambda r, g: r == SEG + k) // 2 + 1, lambda k: u_send(k).start(), k)
         done = last_use(lambda r, g: g == SEG + k) // 2 + 1
         at(done, send_part, k)
         at(done + 1, add_part, k)
-        at(done + 2, lambda k: v_send(k).start(), k)
+    for k in range(SEG):
+        at(last_use(lambda r, g: g == SEG + k) // 2 + 2, lambda k: v_send(k).start(), k)
+    tail_events = [fn for trip in sorted(events) if trip >= NT // 2 - 1 for fn in events[trip]]
 
     def trips(first, last, diag):
-        def body(p, carry):
-            for trip in range(first, last):
-                if trip in events:
-                    @pl.when(p == trip)
-                    def _():
-                        for fn in events[trip]:
-                            fn()
-            step(p, 0, diag)
-            step(p, 1, diag)
-            return carry
-        lax.fori_loop(first, last, body, 0)
+        def body(p, now):
+            for start in range(first, last, 8):
+                inside = [trip for trip in range(start, min(start + 8, last)) if trip in events]
+
+                @pl.when((p >= start) & (p < start + 8))
+                def _():
+                    for trip in inside:
+                        @pl.when(p == trip)
+                        def _():
+                            for fn in events[trip]:
+                                fn()
+            later = (code_at(p + 1, 0), code_at(p + 1, 1))
+            step(now, later, 0, diag)
+            step(now, later, 1, diag)
+            return later
+
+        lax.fori_loop(first, last, body, (jnp.int32(code_at(first, 0)), jnp.int32(code_at(first, 1))))
 
     for k in range(2):
         own(k).wait_recv()
-        for piece in sim_pieces(0, k):
+        for piece in sim_pieces(code_at(0, k), k):
             piece()
         if k == 0:
-            for piece in weight_pieces(0, 0, 1, True):
+            for piece in weight_pieces(code_at(0, 0), 0, 1, True):
                 piece()
     last = NT // 2 - 1
     trips(0, DIAG_TRIPS, True)
     trips(DIAG_TRIPS, last, False)
-    assert max(events) < last
-    for piece in grad_pieces(last, 0) + weight_pieces(last, 1, 1, False) + grad_pieces(last, 1):
+    for piece in (grad_pieces(code_at(last, 0), 0) + weight_pieces(code_at(last, 1), 1, 1, False)
+                  + grad_pieces(code_at(last, 1), 1)):
         piece()
-    for k in range(SEG):
-        b_send(k).start()
-    for k in range(SEG + 1):
-        store(k).start()
+    for fn in tail_events:
+        fn()
+
+    early = SEG - 1
+
+    def fetch(src, k, slot):
+        return pltpu.make_async_copy(src.at[:, pl.ds(k * HALF, HALF)], v_part.at[slot], in_sem.at[slot])
+
+    jobs = []
+    for k in range(early):
+        jobs += [(u_send, u_in, k), (v_send, v_in, k)]
+        if k < SEG - 2:
+            jobs.append((b_send, vp_in, k))
+    jobs += [(b_send, vp_in, k) for k in range(SEG - 2, SEG)]
+
+    def begin(j):
+        make, src, k = jobs[j]
+        make(k).wait_recv()
+        fetch(src, k, j % 2).start()
+
+    def put(k, is_txt):
+        if is_txt:
+            return pltpu.make_async_copy(v_all.at[:, pl.ds(k * TC, HALF)], v_out.at[:, pl.ds(k * HALF, HALF)],
+                                         out_sem.at[k])
+        return pltpu.make_async_copy(u_all.at[:, pl.ds(k * TR, TR)], u_out.at[:, pl.ds(k * TR, TR)],
+                                     out_sem.at[SEG + k])
+
+    begin(0)
+    for j, (make, src, k) in enumerate(jobs):
+        fetch(src, k, j % 2).wait()
+        if j + 1 < len(jobs):
+            begin(j + 1)
+        if make is u_send:
+            u_all[:, k * TR:(k + 1) * TR] += v_part[j % 2]
+        else:
+            v_all[:, k * TC:k * TC + HALF] += v_part[j % 2]
     total = stats[:, :, :LANE]
     for c in range(LANE, HC, LANE):
         total += stats[:, :, c:c + LANE]
     for k in range(3):
         total = swap(k, total)
+    for k in range(SEG):
+        put(k, False).start()
+        put(k, True).start()
     for q in range(4):
         sums_out[q] = jnp.sum(total[q])
-    for k in range(SEG + 1):
-        store(k).wait()
+    for k in range(SEG):
+        put(k, False).wait()
+        put(k, True).wait()
     for k in range(SEG):
         img(k).wait_send()
         own(k).wait_send()
@@ -329,10 +392,12 @@
         fwd(k).wait_send()
         q_send(k).wait_send()
         for copy in (u_send(k), v_send(k), b_send(k)):
-            copy.wait()
-
-
-def finish(temp, img, txt, u_own, u_in, v_own, vp_in, v_in, img_out, txt_out):
+            copy.wait_send()
+    u_send(early).wait_recv()
+    v_send(early).wait_recv()
+
+
+def finish(first_late, temp, img, txt, u_own, u_in, v_own, v_in, img_out, txt_out):
     def project(emb, total, out):
         emb32 = emb[...].astype(F32)
         inv_norm = lax.rsqrt(jnp.sum(emb32 * emb32, axis=-1, keepdims=True))
@@ -341,8 +406,17 @@
         radial = jnp.sum(unit_rows * grad_dir, axis=-1, keepdims=True)
         out[...] = (grad_dir - unit_rows * radial) * inv_norm
 
-    project(img, u_own[...] + u_in[...], img_out)
-    project(txt, (v_own[...] + vp_in[...]) + v_in[...], txt_out)
+    late = pl.program_id(0) >= first_late
+
+    @pl.when(late)
+    def _():
+        project(img, u_own[...] + u_in[...], img_out)
+        project(txt, v_own[...] + v_in[...], txt_out)
+
+    @pl.when(jnp.logical_not(late))
+    def _():
+        project(img, u_own[...], img_out)
+        project(txt, v_own[...], txt_out)
 
 
 def solution(mesh):
@@ -358,7 +432,7 @@
         any_spec = pl.BlockSpec(memory_space=pl.ANY)
         smem_spec = pl.BlockSpec(memory_space=pltpu.SMEM)
         dma = pltpu.SemaphoreType.DMA
-        u_own, v_own, u_in, v_in, vp_in, sums = pl.pallas_call(
+        u_own, v_own, u_in, v_in, _, sums = pl.pallas_call(
             kernel,
             out_shape=[half_out] * 5 + [jax.ShapeDtypeStruct((4,), F32)],
             in_specs=[smem_spec] + [any_spec] * 2,
@@ -379,22 +453,24 @@
                 pltpu.VMEM((2, dim, HALF), F32),
                 dma((kblk,)),
                 dma((SEG * kblk,)),
-            ] + [dma((SEG,))] * 16 + [dma((SEG + 1,)), dma((3,)), dma((3,)), pltpu.SemaphoreType.REGULAR],
+            ] + [dma((SEG,))] * 16 + [dma((2 * SEG,)), dma((3,)), dma((3,)), dma((2,)), pltpu.SemaphoreType.REGULAR],
             compiler_params=pltpu.CompilerParams(
                 collective_id=0, has_side_effects=True, vmem_limit_bytes=67043328),
         )(scal, img_emb, txt_emb)
         sums = sums / total_rows
         loss = LN2 * sums[0] + (sums[2] - sums[1])
         step_rows = 256
+        first_late = (SEG - 1) * TR // step_rows
         emb_spec = pl.BlockSpec((step_rows, dim), lambda i: (i, 0))
         col_spec = pl.BlockSpec((dim, step_rows), lambda i: (0, i))
+        late_spec = pl.BlockSpec((dim, step_rows), lambda i: (0, jnp.maximum(i, first_late)))
         grad_img, grad_txt = pl.pallas_call(
-            finish,
+            functools.partial(finish, first_late),
             grid=(rows // step_rows,),
             out_shape=[jax.ShapeDtypeStruct((rows, dim), F32)] * 2,
-            in_specs=[smem_spec] + [emb_spec] * 2 + [col_spec] * 5,
+            in_specs=[smem_spec] + [emb_spec] * 2 + [col_spec, late_spec] * 2,
             out_specs=[emb_spec] * 2,
-        )(temp_scale[None], img_emb, txt_emb, u_own, u_in, v_own, vp_in, v_in)
+        )(temp_scale[None], img_emb, txt_emb, u_own, u_in, v_own, v_in)
         return loss, grad_img, grad_txt, temp_scale * sums[3], sums[2]
 
     return jax.shard_map(

time: 230 us -> 225 us (0.978)
  Pallas kernels: 222 us -> 216 us
    pallas_call x1, Pallas kernels: 205 us -> 201 us  [local_fn(): pl.pallas_call(kernel, out_shape=[half_out] * 5 + [jax.ShapeDtypeStruct((...]
where the time goes in v3:
time: 225 us
  Pallas kernels  216 us (96%)
  between operations  6.83 us (3%)
    pallas_call x1, Pallas kernels, local_fn(): pl.pallas_call(kernel, out_shape=[half_out] * 5 + [jax.ShapeDtypeStruct((...  201 us
    pallas_call x1, Pallas kernels, local_fn(): pl.pallas_call(functools.partial(finish, first_late), grid=(rows // step_...  14.7 us

profile of v3, /device:TPU:0, one launch (start us, length us, event | category | flops | bytes accessed | tf_op | source)
XLA Modules:
  0.0 224.6 jit_solution(400470693005984530)
XLA Ops:
  2.0 0.6 pad_maximum_fusion.scal
  2.6 201.3 %shard_map.83 = (f32[640,2048]{1,0:T(8,128)}, f32[640,2048]{1,0:T(8,128)}, f32[640,2048]{1,0:T(8,128)}, f32[640,2048]{1,0:T(8,128)}, f32[640,2048]{1,0:T(8,128)}, /*index=5*/f32[4]{0:T(128)}) custom-call(f32[2]{0:T(128)} %pad_maximum_fusion.scal, bf16[2048,640]{1,0:T(8,128)(2,1)} %img.1, bf16[2048,640]{1,0:T(8,128)(2,1)} %txt.1), custom_call_target="tpu_custom_call" | custom-call | tf_op jit(solution)/shard_map/pallas_call | solution.py:435
  203.9 0.6 broadcast_multiply_fusion
  204.5 0.6 fusion
  207.7 14.7 %shard_map.84 = (f32[2048,640]{1,0:T(8,128)}, f32[2048,640]{1,0:T(8,128)}) custom-call(f32[1]{0:T(128)} %bitcast.5.temp, bf16[2048,640]{1,0:T(8,128)(2,1)} %img.1, bf16[2048,640]{1,0:T(8,128)(2,1)} %txt.1, f32[640,2048]{1,0:T(8,128)} %get-tuple-element.13.u_own, f32[640,2048]{1,0:T(8,128)} %get-tuple-element.14.u_in, f32[640,2048]{1,0:T(8,128)} %get-tuple-element.15.v_own, ...), custom_call_target="tpu_custom_call" | custom-call | tf_op jit(solution)/shard_map/pallas_call | solution.py:467

commit v4 on v3

--- a/solution.py
+++ b/solution.py
@@ -14,7 +14,7 @@
 CLAMP = 64.0
 TR, TC, LANE = 512, 1024, 128
 HALF = TC // 2
-HR, HC = 64, 256
+HR, HC = 64, 128
 SEG = 4
 
 ORDER = [
@@ -51,7 +51,7 @@
     return min(t for t, rg in enumerate(ORDER) if match(*rg))
 
 
-def kernel(scal, img_hbm, txt_hbm, u_out, v_out, u_in, v_in, vp_in, sums_out, stats, st_buf, st_in, x_all, xt_all, yt_all, u_all, v_all,
+def kernel(total_rows, scal, img_hbm, txt_hbm, u_out, v_out, u_in, v_in, vp_in, loss_out, temp_out, bias_out, stats, st_buf, st_in, x_all, xt_all, yt_all, u_all, v_all,
            s0, s1, h0, h1, v_part, x_sem, y_sem, img_s, img_r, own_s, own_r, col_s, col_r, fwd_s, fwd_r, u_s, u_r,
            q_s, q_r, v_s, v_r, b_s, b_r, out_sem, st_s, st_r, in_sem, free_sem):
     me = lax.axis_index('dp')
@@ -175,7 +175,7 @@
         img(k).start()
         own(k).start()
 
-    scale2, bias2 = scal[0], scal[1]
+    scale2, bias2 = scal[0] * LOG2E, scal[1] * LOG2E
     stats[...] = jnp.zeros_like(stats)
     v_all[...] = jnp.zeros_like(v_all)
 
@@ -364,6 +364,15 @@
                                      out_sem.at[SEG + k])
 
     begin(0)
+    total = stats[:, :, :LANE]
+    for c in range(LANE, HC, LANE):
+        total += stats[:, :, c:c + LANE]
+    for k in range(3):
+        total = swap(k, total)
+    sums = [jnp.sum(total[q]) / total_rows for q in range(4)]
+    loss_out[0] = LN2 * sums[0] + (sums[2] - sums[1])
+    temp_out[0] = scal[0] * sums[3]
+    bias_out[0] = sums[2]
     for j, (make, src, k) in enumerate(jobs):
         fetch(src, k, j % 2).wait()
         if j + 1 < len(jobs):
@@ -372,16 +381,10 @@
             u_all[:, k * TR:(k + 1) * TR] += v_part[j % 2]
         else:
             v_all[:, k * TC:k * TC + HALF] += v_part[j % 2]
-    total = stats[:, :, :LANE]
-    for c in range(LANE, HC, LANE):
-        total += stats[:, :, c:c + LANE]
-    for k in range(3):
-        total = swap(k, total)
-    for k in range(SEG):
-        put(k, False).start()
-        put(k, True).start()
-    for q in range(4):
-        sums_out[q] = jnp.sum(total[q])
+        rest = [job[2] for job in jobs[j + 1:] if (job[0] is u_send) == (make is u_send)]
+        if k not in rest:
+            put(k, make is not u_send).start()
+    put(early, False).start()
     for k in range(SEG):
         put(k, False).wait()
         put(k, True).wait()
@@ -397,12 +400,12 @@
     v_send(early).wait_recv()
 
 
-def finish(first_late, temp, img, txt, u_own, u_in, v_own, v_in, img_out, txt_out):
+def finish(first_late, scal, img, txt, u_own, u_in, v_own, v_in, img_out, txt_out):
     def project(emb, total, out):
         emb32 = emb[...].astype(F32)
         inv_norm = lax.rsqrt(jnp.sum(emb32 * emb32, axis=-1, keepdims=True))
         unit_rows = emb32 * inv_norm
-        grad_dir = (total * temp[0]).T
+        grad_dir = (total * scal[0]).T
         radial = jnp.sum(unit_rows * grad_dir, axis=-1, keepdims=True)
         out[...] = (grad_dir - unit_rows * radial) * inv_norm
 
@@ -425,18 +428,17 @@
     def local_fn(img_emb, txt_emb, log_temp, logit_bias):
         rows, dim = img_emb.shape
         total_rows = rows * group_size
-        temp_scale = jnp.exp(log_temp)
-        scal = jnp.stack([temp_scale * LOG2E, logit_bias * LOG2E])
+        scal = jnp.stack([jnp.exp(log_temp), logit_bias])
         nblk, kblk = rows // LANE, dim // LANE
         half_out = jax.ShapeDtypeStruct((dim, rows), F32)
         any_spec = pl.BlockSpec(memory_space=pl.ANY)
         smem_spec = pl.BlockSpec(memory_space=pltpu.SMEM)
         dma = pltpu.SemaphoreType.DMA
-        u_own, v_own, u_in, v_in, _, sums = pl.pallas_call(
-            kernel,
-            out_shape=[half_out] * 5 + [jax.ShapeDtypeStruct((4,), F32)],
+        u_own, v_own, u_in, v_in, _, loss, grad_temp, grad_bias = pl.pallas_call(
+            functools.partial(kernel, float(total_rows)),
+            out_shape=[half_out] * 5 + [jax.ShapeDtypeStruct((1,), F32)] * 3,
             in_specs=[smem_spec] + [any_spec] * 2,
-            out_specs=[any_spec] * 5 + [smem_spec],
+            out_specs=[any_spec] * 5 + [smem_spec] * 3,
             scratch_shapes=[
                 pltpu.VMEM((4, 8, HC), F32),
                 pltpu.VMEM((3, 4, 8, LANE), F32),
@@ -457,8 +459,6 @@
             compiler_params=pltpu.CompilerParams(
                 collective_id=0, has_side_effects=True, vmem_limit_bytes=67043328),
         )(scal, img_emb, txt_emb)
-        sums = sums / total_rows
-        loss = LN2 * sums[0] + (sums[2] - sums[1])
         step_rows = 256
         first_late = (SEG - 1) * TR // step_rows
         emb_spec = pl.BlockSpec((step_rows, dim), lambda i: (i, 0))
@@ -470,8 +470,8 @@
             out_shape=[jax.ShapeDtypeStruct((rows, dim), F32)] * 2,
             in_specs=[smem_spec] + [emb_spec] * 2 + [col_spec, late_spec] * 2,
             out_specs=[emb_spec] * 2,
-        )(temp_scale[None], img_emb, txt_emb, u_own, u_in, v_own, v_in)
-        return loss, grad_img, grad_txt, temp_scale * sums[3], sums[2]
+        )(scal, img_emb, txt_emb, u_own, u_in, v_own, v_in)
+        return loss[0], grad_img, grad_txt, grad_temp[0], grad_bias[0]
 
     return jax.shard_map(
         local_fn,

time: 225 us -> 237 us (1.053)
  Pallas kernels: 216 us -> 229 us
    pallas_call x1, Pallas kernels: 201 us -> 214 us  [local_fn(): pl.pallas_call(functools.partial(kernel, float(total_rows)), out_shape=[h...]
where the time goes in v4:
time: 237 us; the launch traced here: 236 us
  Pallas kernels  229 us (97%)
  between operations  7.3 us (3%)
    pallas_call x1, Pallas kernels, local_fn(): pl.pallas_call(functools.partial(kernel, float(total_rows)), out_shape=[h...  214 us
    pallas_call x1, Pallas kernels, local_fn(): pl.pallas_call(functools.partial(finish, first_late), grid=(rows // step_...  14.7 us

profile of v4, /device:TPU:0, one launch (start us, length us, event | category | flops | bytes accessed | tf_op | source)
XLA Modules:
  0.0 236.5 jit_solution(17377821148071139854)
XLA Ops:
  2.0 0.6 pad_maximum_fusion.scal
  2.5 213.9 %shard_map.83 = (f32[640,2048]{1,0:T(8,128)}, f32[640,2048]{1,0:T(8,128)}, f32[640,2048]{1,0:T(8,128)}, f32[640,2048]{1,0:T(8,128)}, f32[640,2048]{1,0:T(8,128)}, /*index=5*/f32[1]{0:T(128)}, f32[1]{0:T(128)}, f32[1]{0:T(128)}) custom-call(f32[2]{0:T(128)} %pad_maximum_fusion.scal, bf16[2048,640]{1,0:T(8,128)(2,1)} %img.1, bf16[2048,640]{1,0:T(8,128)(2,1)} %txt.1), custom_call_target="tpu_custom_call" | custom-call | tf_op jit(solution)/shard_map/pallas_call | solution.py:437
  216.4 14.7 %shard_map.84 = (f32[2048,640]{1,0:T(8,128)}, f32[2048,640]{1,0:T(8,128)}) custom-call(f32[2]{0:T(128)} %pad_maximum_fusion.scal, bf16[2048,640]{1,0:T(8,128)(2,1)} %img.1, bf16[2048,640]{1,0:T(8,128)(2,1)} %txt.1, f32[640,2048]{1,0:T(8,128)} %get-tuple-element.15.u_own, f32[640,2048]{1,0:T(8,128)} %get-tuple-element.16.u_in, ...), custom_call_target="tpu_custom_call" | custom-call | tf_op jit(solution)/shard_map/pallas_call | solution.py:467

commit v5 on v4

--- a/solution.py
+++ b/solution.py
@@ -55,7 +55,7 @@
            s0, s1, h0, h1, v_part, x_sem, y_sem, img_s, img_r, own_s, own_r, col_s, col_r, fwd_s, fwd_r, u_s, u_r,
            q_s, q_r, v_s, v_r, b_s, b_r, out_sem, st_s, st_r, in_sem, free_sem):
     me = lax.axis_index('dp')
-    core_nbr, row_nbr, col_nbr = me ^ 1, me ^ 2, me ^ 4
+    core_nbr, row_nbr, col_nbr, far_nbr = me ^ 1, me ^ 2, me ^ 4, me ^ 6
     dim = u_all.shape[0]
     rows = img_hbm.shape[0]
     nblk = rows // LANE
@@ -63,7 +63,7 @@
     kblk = dim // LANE
 
     barrier = pltpu.get_barrier_semaphore()
-    for nbr in (core_nbr, row_nbr, col_nbr):
+    for nbr in (core_nbr, row_nbr, col_nbr, far_nbr):
         pl.semaphore_signal(barrier, inc=1, device_id=(nbr,), device_id_type=MESH)
 
     def remote(src, dst, s, r, k, dev):
@@ -104,34 +104,8 @@
         return pltpu.make_async_copy(txt_hbm.at[pl.ds(k * TR, TR), pl.ds(kb * LANE, LANE)],
                                      wgt[k % 2].at[kb], y_sem.at[k * kblk + kb])
 
-    def swap(k, value):
-        nbr = (core_nbr, row_nbr, col_nbr)[k]
-        st_buf[k] = value
-        copy = remote(st_buf.at[k], st_in.at[k], st_s, st_r, k, nbr)
-        copy.start()
-        copy.wait()
-        return st_buf[k] + st_in[k]
-
-    def load_img(kb):
-        return pltpu.make_async_copy(img_hbm.at[:, pl.ds(kb * LANE, LANE)], x_all.at[kb, pl.ds(0, rows)], x_sem.at[kb])
-
-    def load_txt(k, kb):
-        return pltpu.make_async_copy(txt_hbm.at[pl.ds(k * TR, TR), pl.ds(kb * LANE, LANE)],
-                                     wgt[k % 2].at[kb], y_sem.at[k * kblk + kb])
-
-    def swap(k, value):
-        nbr = (core_nbr, row_nbr, col_nbr)[k]
-        st_buf[k] = value
-        copy = remote(st_buf.at[k], st_in.at[k], st_s, st_r, k, nbr)
-        copy.start()
-        copy.wait()
-        return st_buf[k] + st_in[k]
-
-    def store(k):
-        if k < SEG:
-            return pltpu.make_async_copy(v_all.at[:, pl.ds(k * TC, HALF)], v_out.at[:, pl.ds(k * HALF, HALF)],
-                                         out_sem.at[k])
-        return pltpu.make_async_copy(u_all.at[:, pl.ds(0, rows)], u_out, out_sem.at[k])
+    def stat_copy(k):
+        return remote(st_buf.at[min(k, 1)], st_in.at[k], st_s, st_r, k, (core_nbr, row_nbr, col_nbr, far_nbr)[k])
 
     sim, wgt = (s0, s1), (h0, h1)
     for kb in range(kblk):
@@ -170,7 +144,7 @@
             x_all[kb, at_rows, :] = block
             put_transposed(xt_all, k * (TR // LANE), kb, block)
         if k == 0:
-            pl.semaphore_wait(barrier, 3)
+            pl.semaphore_wait(barrier, 4)
         col(k).start()
         img(k).start()
         own(k).start()
@@ -367,12 +341,8 @@
     total = stats[:, :, :LANE]
     for c in range(LANE, HC, LANE):
         total += stats[:, :, c:c + LANE]
-    for k in range(3):
-        total = swap(k, total)
-    sums = [jnp.sum(total[q]) / total_rows for q in range(4)]
-    loss_out[0] = LN2 * sums[0] + (sums[2] - sums[1])
-    temp_out[0] = scal[0] * sums[3]
-    bias_out[0] = sums[2]
+    st_buf[0] = total
+    stat_copy(0).start()
     for j, (make, src, k) in enumerate(jobs):
         fetch(src, k, j % 2).wait()
         if j + 1 < len(jobs):
@@ -384,7 +354,19 @@
         rest = [job[2] for job in jobs[j + 1:] if (job[0] is u_send) == (make is u_send)]
         if k not in rest:
             put(k, make is not u_send).start()
+        if j == 5:
+            stat_copy(0).wait()
+            st_buf[1] = st_buf[0] + st_in[0]
+            for q in range(1, 4):
+                stat_copy(q).start()
     put(early, False).start()
+    for q in range(1, 4):
+        stat_copy(q).wait()
+    total = (st_buf[1] + st_in[1]) + (st_in[2] + st_in[3])
+    sums = [jnp.sum(total[q]) / total_rows for q in range(4)]
+    loss_out[0] = LN2 * sums[0] + (sums[2] - sums[1])
+    temp_out[0] = scal[0] * sums[3]
+    bias_out[0] = sums[2]
     for k in range(SEG):
         put(k, False).wait()
         put(k, True).wait()
@@ -441,8 +423,8 @@
             out_specs=[any_spec] * 5 + [smem_spec] * 3,
             scratch_shapes=[
                 pltpu.VMEM((4, 8, HC), F32),
-                pltpu.VMEM((3, 4, 8, LANE), F32),
-                pltpu.VMEM((3, 4, 8, LANE), F32),
+                pltpu.VMEM((2, 4, 8, LANE), F32),
+                pltpu.VMEM((4, 4, 8, LANE), F32),
                 pltpu.VMEM((kblk, 2 * rows, LANE), BF16),
                 pltpu.VMEM((2 * nblk, dim, LANE), BF16),
                 pltpu.VMEM((4 * nblk, dim, LANE), BF16),
@@ -455,7 +437,7 @@
                 pltpu.VMEM((2, dim, HALF), F32),
                 dma((kblk,)),
                 dma((SEG * kblk,)),
-            ] + [dma((SEG,))] * 16 + [dma((2 * SEG,)), dma((3,)), dma((3,)), dma((2,)), pltpu.SemaphoreType.REGULAR],
+            ] + [dma((SEG,))] * 16 + [dma((2 * SEG,)), dma((4,)), dma((4,)), dma((2,)), pltpu.SemaphoreType.REGULAR],
             compiler_params=pltpu.CompilerParams(
                 collective_id=0, has_side_effects=True, vmem_limit_bytes=67043328),
         )(scal, img_emb, txt_emb)

time: 237 us -> 219 us (0.924)
  Pallas kernels: 229 us -> 211 us
    pallas_call x1, Pallas kernels: 214 us -> 196 us  [local_fn(): pl.pallas_call(functools.partial(kernel, float(total_rows)), out_shape=[h...]
where the time goes in v5:
time: 219 us; the launch traced here: 218 us
  Pallas kernels  211 us (96%)
  between operations  7.3 us (3%)
    pallas_call x1, Pallas kernels, local_fn(): pl.pallas_call(functools.partial(kernel, float(total_rows)), out_shape=[h...  196 us
    pallas_call x1, Pallas kernels, local_fn(): pl.pallas_call(functools.partial(finish, first_late), grid=(rows // step_...  14.7 us

profile of v5, /device:TPU:0, one launch (start us, length us, event | category | flops | bytes accessed | tf_op | source)
XLA Modules:
  0.0 218.4 jit_solution(516904324875885011)
XLA Ops:
  2.0 0.6 pad_maximum_fusion.scal
  2.5 195.8 %shard_map.83 = (f32[640,2048]{1,0:T(8,128)}, f32[640,2048]{1,0:T(8,128)}, f32[640,2048]{1,0:T(8,128)}, f32[640,2048]{1,0:T(8,128)}, f32[640,2048]{1,0:T(8,128)}, /*index=5*/f32[1]{0:T(128)}, f32[1]{0:T(128)}, f32[1]{0:T(128)}) custom-call(f32[2]{0:T(128)} %pad_maximum_fusion.scal, bf16[2048,640]{1,0:T(8,128)(2,1)} %img.1, bf16[2048,640]{1,0:T(8,128)(2,1)} %txt.1), custom_call_target="tpu_custom_call" | custom-call | tf_op jit(solution)/shard_map/pallas_call | solution.py:419
  198.4 14.7 %shard_map.84 = (f32[2048,640]{1,0:T(8,128)}, f32[2048,640]{1,0:T(8,128)}) custom-call(f32[2]{0:T(128)} %pad_maximum_fusion.scal, bf16[2048,640]{1,0:T(8,128)(2,1)} %img.1, bf16[2048,640]{1,0:T(8,128)(2,1)} %txt.1, f32[640,2048]{1,0:T(8,128)} %get-tuple-element.15.u_own, f32[640,2048]{1,0:T(8,128)} %get-tuple-element.16.u_in, ...), custom_call_target="tpu_custom_call" | custom-call | tf_op jit(solution)/shard_map/pallas_call | solution.py:449
